TPU v7x, 32 devices: a 4x2x2 block of a 4x4x8 slice. The times are simulated.
32 devices in a mesh: data: 4 (over y, z), ctx: 8 (over x, core).
Axes of the slice: x: 4, y: 2, z: 2, core: 2. Of those that a mesh axis runs over, the one named last changes fastest.
The devices are a block of a 4x4x8 slice.
Arguments:
- queries: bfloat16 [32, 6144, 3, 128], P('data', 'ctx'), parts along dimension 0
- keys_in: bfloat16 [32, 6144, 1, 128], P('data', 'ctx'), parts along dimension 0
- values_in: bfloat16 [32, 6144, 1, 128], P('data', 'ctx'), parts along dimension 0
- grad_out: bfloat16 [32, 6144, 3, 128], P('data', 'ctx'), parts along dimension 0
Outputs:
- output 1: bfloat16 [32, 6144, 3, 128], P('data', 'ctx'), parts along dimension 0
- output 2: bfloat16 [32, 6144, 3, 128], P('data', 'ctx'), parts along dimension 0
- output 3: bfloat16 [32, 6144, 1, 128], P('data', 'ctx'), parts along dimension 0
- output 4: bfloat16 [32, 6144, 1, 128], P('data', 'ctx'), parts along dimension 0
There are 4 independent parts. A program takes and returns all parts, laid end to end along the dimension named above; each array names one.
All inputs are finite; a program needn't handle non-finite values.
Results may differ from a plain program's by a relative error of at most 0.0171527.
Values are sent between devices in bfloat16 or wider.
A program may use at most 768 MiB of HBM per device.

v0:
```python
import jax
import jax.numpy as jnp
from jax import lax
from jax.sharding import PartitionSpec as P

MASK_VALUE = -1e30


def solution(mesh):
    ctx_size = mesh.shape["ctx"]
    block_spec = P("data", "ctx", None, None)
    perm_next = [(dev_id, (dev_id + 1) % ctx_size) for dev_id in range(ctx_size)]

    def local_attention(queries, keys_in, values_in, grad_out):
        batch_size, shard_len, q_heads, head_dim = queries.shape
        kv_heads = keys_in.shape[2]
        group_size = q_heads // kv_heads
        half_len = shard_len // 2
        score_scale = head_dim ** -0.5
        my_index = lax.axis_index("ctx")
        q_five = queries.reshape(batch_size, shard_len, kv_heads, group_size, head_dim)
        g_five = grad_out.reshape(batch_size, shard_len, kv_heads, group_size, head_dim)
        own_mask = jnp.arange(shard_len)[:, None] >= jnp.arange(shard_len)[None, :]

        def scores_of(q_blk, k_blk, mask_tile):
            raw_scores = jnp.einsum("bqhgd,bkhd->bhgqk", q_blk, k_blk, preferred_element_type=jnp.float32) * score_scale
            if mask_tile is None:
                return raw_scores
            return jnp.where(mask_tile, raw_scores, MASK_VALUE)

        def fwd_update(run_state, q_blk, k_blk, v_blk, mask_tile):
            run_max, run_sum, acc_out = run_state
            scores = scores_of(q_blk, k_blk, mask_tile)
            new_max = jnp.maximum(run_max, jnp.max(scores, axis=-1))
            prob_tile = jnp.exp(scores - new_max[..., None])
            decay_factor = jnp.exp(run_max - new_max)
            new_sum = run_sum * decay_factor + jnp.sum(prob_tile, axis=-1)
            pv_part = jnp.einsum("bhgqk,bkhd->bhgqd", prob_tile.astype(jnp.bfloat16), v_blk, preferred_element_type=jnp.float32)
            return new_max, new_sum, acc_out * decay_factor[..., None] + pv_part

        def fwd_past(op_args):
            run_state, k_cur, v_cur = op_args
            return fwd_update(run_state, q_five, k_cur[:, :half_len], v_cur[:, :half_len], None)

        def fwd_future(op_args):
            run_state, k_cur, v_cur = op_args
            low_half = tuple(tensor[:, :, :, :half_len] for tensor in run_state)
            high_half = tuple(tensor[:, :, :, half_len:] for tensor in run_state)
            high_half = fwd_update(high_half, q_five[:, half_len:], k_cur, v_cur, None)
            return tuple(jnp.concatenate([low_part, high_part], axis=3) for low_part, high_part in zip(low_half, high_half))

        def fwd_step(step_idx, loop_carry):
            k_cur, v_cur, run_state = loop_carry
            k_cur = lax.ppermute(k_cur, "ctx", perm_next)
            v_cur = lax.ppermute(v_cur, "ctx", perm_next)
            source_id = (my_index - step_idx) % ctx_size
            run_state = lax.cond(source_id < my_index, fwd_past, fwd_future, (run_state, k_cur, v_cur))
            return k_cur, v_cur, run_state

        stat_shape = (batch_size, kv_heads, group_size, shard_len)
        run_state = (jnp.full(stat_shape, MASK_VALUE, jnp.float32), jnp.zeros(stat_shape, jnp.float32), jnp.zeros(stat_shape + (head_dim,), jnp.float32))
        run_state = fwd_update(run_state, q_five, keys_in, values_in, own_mask)
        loop_out = lax.fori_loop(1, ctx_size, fwd_step, (keys_in, values_in, run_state))
        run_max, run_sum, acc_out = loop_out[2]
        out_heads = (acc_out / run_sum[..., None]).astype(jnp.bfloat16)
        log_sum = run_max + jnp.log(run_sum)
        attn_out = jnp.transpose(out_heads, (0, 3, 1, 2, 4)).reshape(batch_size, shard_len, q_heads, head_dim)
        d_rows = jnp.einsum("bqhgd,bhgqd->bhgq", g_five, out_heads, preferred_element_type=jnp.float32)

        def bwd_block(q_blk, g_blk, lse_blk, drow_blk, k_blk, v_blk, mask_tile):
            prob_tile = jnp.exp(scores_of(q_blk, k_blk, mask_tile) - lse_blk[..., None])
            grad_v = jnp.einsum("bhgqk,bqhgd->bkhd", prob_tile.astype(jnp.bfloat16), g_blk, preferred_element_type=jnp.float32)
            dprob_tile = jnp.einsum("bqhgd,bkhd->bhgqk", g_blk, v_blk, preferred_element_type=jnp.float32)
            dscore_tile = (prob_tile * (dprob_tile - drow_blk[..., None])).astype(jnp.bfloat16)
            grad_q = jnp.einsum("bhgqk,bkhd->bqhgd", dscore_tile, k_blk, preferred_element_type=jnp.float32) * score_scale
            grad_k = jnp.einsum("bhgqk,bqhgd->bkhd", dscore_tile, q_blk, preferred_element_type=jnp.float32) * score_scale
            return grad_q, grad_k, grad_v

        def bwd_past(op_args):
            dq_acc, dk_acc, dv_acc, k_cur, v_cur = op_args
            grad_q, grad_k, grad_v = bwd_block(q_five, g_five, log_sum, d_rows, k_cur[:, :half_len], v_cur[:, :half_len], None)
            dk_acc = jnp.concatenate([dk_acc[:, :half_len] + grad_k, dk_acc[:, half_len:]], axis=1)
            dv_acc = jnp.concatenate([dv_acc[:, :half_len] + grad_v, dv_acc[:, half_len:]], axis=1)
            return dq_acc + grad_q, dk_acc, dv_acc

        def bwd_future(op_args):
            dq_acc, dk_acc, dv_acc, k_cur, v_cur = op_args
            grad_q, grad_k, grad_v = bwd_block(q_five[:, half_len:], g_five[:, half_len:], log_sum[..., half_len:], d_rows[..., half_len:], k_cur, v_cur, None)
            dq_acc = jnp.concatenate([dq_acc[:, :half_len], dq_acc[:, half_len:] + grad_q], axis=1)
            return dq_acc, dk_acc + grad_k, dv_acc + grad_v

        def bwd_step(step_idx, loop_carry):
            dq_acc, dk_acc, dv_acc, k_cur, v_cur = loop_carry
            k_cur = lax.ppermute(k_cur, "ctx", perm_next)
            v_cur = lax.ppermute(v_cur, "ctx", perm_next)
            dk_acc = lax.ppermute(dk_acc, "ctx", perm_next)
            dv_acc = lax.ppermute(dv_acc, "ctx", perm_next)
            source_id = (my_index - step_idx) % ctx_size
            dq_acc, dk_acc, dv_acc = lax.cond(source_id < my_index, bwd_past, bwd_future, (dq_acc, dk_acc, dv_acc, k_cur, v_cur))
            return dq_acc, dk_acc, dv_acc, k_cur, v_cur

        first_grads = bwd_block(q_five, g_five, log_sum, d_rows, keys_in, values_in, own_mask)
        loop_out = lax.fori_loop(1, ctx_size, bwd_step, first_grads + (keys_in, values_in))
        grad_k = lax.ppermute(loop_out[1], "ctx", perm_next)
        grad_v = lax.ppermute(loop_out[2], "ctx", perm_next)
        grad_q = loop_out[0].reshape(batch_size, shard_len, q_heads, head_dim).astype(jnp.bfloat16)
        return attn_out, grad_q, grad_k.astype(jnp.bfloat16), grad_v.astype(jnp.bfloat16)

    return jax.shard_map(local_attention, mesh=mesh, in_specs=(block_spec,) * 4, out_specs=(block_spec,) * 4, check_vma=False)
```

profile of v0, /device:TPU:81, one launch (start us, length us, event | category | flops | bytes accessed | tf_op | source)
XLA Modules:
  0.0 2190.3 jit_solution(9668697380136752377)
XLA Ops:
  76.9 674.6 %while.46 = (s32[]{:T(128)}, bf16[8,768,1,128]{3,1,0,2:T(8,128)(2,1)}, bf16[8,768,1,128]{3,1,0,2:T(8,128)(2,1)}, f32[8,1,3,768]{3,2,0,1:T(4,128)S(1)}, f32[8,1,3...) while((s32[]{:T(128)}, ...), condition=%wide.region_9.10_spmd, body=%wide.region_2.9_spmd.sunk | while | flops 3685284864 | bytes 196239920 | solution.py:63
  114.0 47.4 %conditional.4 = (f32[8,1,3,768]{3,2,0,1:T(4,128)}, f32[8,1,3,768]{3,2,0,1:T(4,128)S(1)}, f32[8,1,3,768,128]{4,3,2,0,1:T(8,128)}) conditional(s32[]{:T(128)} %convert_element_type.123, (f32[8,1,3,768]{3,2,0,1:T(4,128)S(1)}, bf16[8,768,1,128]{3,1,0,2:T(8,128)(2,1)}, bf16[8,768,1,3,128]{4,1,3,0,2:T(8,128)(2,1)}, f32[8,1,3,768]{3,2,0,1:T(4,128)S(1)}, ...), branch_computations={%region_3.5_spmd, %region_6.8_spmd} | conditional | flops 3685284864 | bytes 177217664 | solution.py:57
  204.4 54.8 %conditional.4 = (f32[8,1,3,768]{3,2,0,1:T(4,128)}, f32[8,1,3,768]{3,2,0,1:T(4,128)S(1)}, f32[8,1,3,768,128]{4,3,2,0,1:T(8,128)}) conditional(s32[]{:T(128)} %convert_element_type.123, (f32[8,1,3,768]{3,2,0,1:T(4,128)S(1)}, bf16[8,768,1,128]{3,1,0,2:T(8,128)(2,1)}, bf16[8,768,1,3,128]{4,1,3,0,2:T(8,128)(2,1)}, f32[8,1,3,768]{3,2,0,1:T(4,128)S(1)}, ...), branch_computations={%region_3.5_spmd, %region_6.8_spmd} | conditional | flops 3685284864 | bytes 177217664 | solution.py:57
  299.5 54.8 %conditional.4 = (f32[8,1,3,768]{3,2,0,1:T(4,128)}, f32[8,1,3,768]{3,2,0,1:T(4,128)S(1)}, f32[8,1,3,768,128]{4,3,2,0,1:T(8,128)}) conditional(s32[]{:T(128)} %convert_element_type.123, (f32[8,1,3,768]{3,2,0,1:T(4,128)S(1)}, bf16[8,768,1,128]{3,1,0,2:T(8,128)(2,1)}, bf16[8,768,1,3,128]{4,1,3,0,2:T(8,128)(2,1)}, f32[8,1,3,768]{3,2,0,1:T(4,128)S(1)}, ...), branch_computations={%region_3.5_spmd, %region_6.8_spmd} | conditional | flops 3685284864 | bytes 177217664 | solution.py:57
  397.2 54.8 %conditional.4 = (f32[8,1,3,768]{3,2,0,1:T(4,128)}, f32[8,1,3,768]{3,2,0,1:T(4,128)S(1)}, f32[8,1,3,768,128]{4,3,2,0,1:T(8,128)}) conditional(s32[]{:T(128)} %convert_element_type.123, (f32[8,1,3,768]{3,2,0,1:T(4,128)S(1)}, bf16[8,768,1,128]{3,1,0,2:T(8,128)(2,1)}, bf16[8,768,1,3,128]{4,1,3,0,2:T(8,128)(2,1)}, f32[8,1,3,768]{3,2,0,1:T(4,128)S(1)}, ...), branch_computations={%region_3.5_spmd, %region_6.8_spmd} | conditional | flops 3685284864 | bytes 177217664 | solution.py:57
  494.9 54.8 %conditional.4 = (f32[8,1,3,768]{3,2,0,1:T(4,128)}, f32[8,1,3,768]{3,2,0,1:T(4,128)S(1)}, f32[8,1,3,768,128]{4,3,2,0,1:T(8,128)}) conditional(s32[]{:T(128)} %convert_element_type.123, (f32[8,1,3,768]{3,2,0,1:T(4,128)S(1)}, bf16[8,768,1,128]{3,1,0,2:T(8,128)(2,1)}, bf16[8,768,1,3,128]{4,1,3,0,2:T(8,128)(2,1)}, f32[8,1,3,768]{3,2,0,1:T(4,128)S(1)}, ...), branch_computations={%region_3.5_spmd, %region_6.8_spmd} | conditional | flops 3685284864 | bytes 177217664 | solution.py:57
  592.6 54.8 %conditional.4 = (f32[8,1,3,768]{3,2,0,1:T(4,128)}, f32[8,1,3,768]{3,2,0,1:T(4,128)S(1)}, f32[8,1,3,768,128]{4,3,2,0,1:T(8,128)}) conditional(s32[]{:T(128)} %convert_element_type.123, (f32[8,1,3,768]{3,2,0,1:T(4,128)S(1)}, bf16[8,768,1,128]{3,1,0,2:T(8,128)(2,1)}, bf16[8,768,1,3,128]{4,1,3,0,2:T(8,128)(2,1)}, f32[8,1,3,768]{3,2,0,1:T(4,128)S(1)}, ...), branch_computations={%region_3.5_spmd, %region_6.8_spmd} | conditional | flops 3685284864 | bytes 177217664 | solution.py:57
  690.2 54.8 %conditional.4 = (f32[8,1,3,768]{3,2,0,1:T(4,128)}, f32[8,1,3,768]{3,2,0,1:T(4,128)S(1)}, f32[8,1,3,768,128]{4,3,2,0,1:T(8,128)}) conditional(s32[]{:T(128)} %convert_element_type.123, (f32[8,1,3,768]{3,2,0,1:T(4,128)S(1)}, bf16[8,768,1,128]{3,1,0,2:T(8,128)(2,1)}, bf16[8,768,1,3,128]{4,1,3,0,2:T(8,128)(2,1)}, f32[8,1,3,768]{3,2,0,1:T(4,128)S(1)}, ...), branch_computations={%region_3.5_spmd, %region_6.8_spmd} | conditional | flops 3685284864 | bytes 177217664 | solution.py:57
  787.3 32.3 %fusion.102 = bf16[8,3,768,768]{2,3,1,0:T(8,128)(2,1)} fusion(f32[8,768,768,3]{2,1,3,0:T(8,128)} %get-tuple-element.682, f32[8,3,768]{2,1,0:T(4,128)S(1)} %fusion.109, f32[8,3,768]{2,1,0:T(4,128)S(1)} %bitcast.438, pred[768,768]{0,1:T(8,128)(4,1)S(1)} %copy-done.5, bf16[8,768,3,128]{3,1,2,0:T(8,128)(2,1)S(1)} %bitcast.430, ...), kind=kOutput, calls=%fused_computation.118 | convolution fusion | flops 3708813312 | bytes 91963392 | tf_op jit(solution)/shard_map/bqhgd,bkhd->bhgqk/dot_general | solution.py:73
  852.7 1286.6 %while.47 = (s32[]{:T(128)}, f32[8,768,1,3,128]{4,1,3,0,2:T(8,128)}, f32[8,768,1,128]{3,1,0,2:T(8,128)}, f32[8,768,1,128]{3,1,0,2:T(8,128)}, bf16[8,768,1,128]{3...) while((s32[]{:T(128)}, ...), condition=%wide.region_13.14_spmd, body=%wide.region_10.13_spmd.sunk | while | flops 9123790848 | bytes 278655712 | solution.py:103
  855.7 84.5 %collective-permute-done.2 = bf16[8,768,1,128]{3,1,0,2:T(8,128)(2,1)S(1)} collective-permute-done((bf16[8,768,1,128]{3,1,0,2:T(8,128)(2,1)}, bf16[8,768,1,128]{3,1,0,2:T(8,128)(2,1)S(1)}, u32[]{:S(2)}, u32[]{:S(2)}) %collective-permute-start.2) | collective-permute-done | bytes 1572896 | tf_op jit(solution)/shard_map/while/body/eval_jaxpr/ppermute | solution.py:94
  959.8 74.2 %conditional.5 = (f32[8,768,1,3,128]{4,1,3,0,2:T(8,128)}, f32[8,768,1,128]{3,1,0,2:T(8,128)}, f32[8,768,1,128]{3,1,0,2:T(8,128)}) conditional(s32[]{:T(128)} %convert_element_type.124, (f32[8,768,1,3,128]{4,1,3,0,2:T(8,128)}, bf16[8,768,1,128]{3,1,0,2:T(8,128)(2,1)S(1)}, bf16[8,768,1,3,128]{4,1,3,0,2:T(8,128)(2,1)}, ...), branch_computations={%region_11.11_spmd, %region_12.12_spmd} | conditional | flops 9123790848 | bytes 234614944 | solution.py:99
  1036.7 84.6 %collective-permute-done.2 = bf16[8,768,1,128]{3,1,0,2:T(8,128)(2,1)S(1)} collective-permute-done((bf16[8,768,1,128]{3,1,0,2:T(8,128)(2,1)}, bf16[8,768,1,128]{3,1,0,2:T(8,128)(2,1)S(1)}, u32[]{:S(2)}, u32[]{:S(2)}) %collective-permute-start.2) | collective-permute-done | bytes 1572896 | tf_op jit(solution)/shard_map/while/body/eval_jaxpr/ppermute | solution.py:94
  1140.9 77.8 %conditional.5 = (f32[8,768,1,3,128]{4,1,3,0,2:T(8,128)}, f32[8,768,1,128]{3,1,0,2:T(8,128)}, f32[8,768,1,128]{3,1,0,2:T(8,128)}) conditional(s32[]{:T(128)} %convert_element_type.124, (f32[8,768,1,3,128]{4,1,3,0,2:T(8,128)}, bf16[8,768,1,128]{3,1,0,2:T(8,128)(2,1)S(1)}, bf16[8,768,1,3,128]{4,1,3,0,2:T(8,128)(2,1)}, ...), branch_computations={%region_11.11_spmd, %region_12.12_spmd} | conditional | flops 9123790848 | bytes 234614944 | solution.py:99
  1218.9 84.6 %collective-permute-done.2 = bf16[8,768,1,128]{3,1,0,2:T(8,128)(2,1)S(1)} collective-permute-done((bf16[8,768,1,128]{3,1,0,2:T(8,128)(2,1)}, bf16[8,768,1,128]{3,1,0,2:T(8,128)(2,1)S(1)}, u32[]{:S(2)}, u32[]{:S(2)}) %collective-permute-start.2) | collective-permute-done | bytes 1572896 | tf_op jit(solution)/shard_map/while/body/eval_jaxpr/ppermute | solution.py:94
  1323.0 77.8 %conditional.5 = (f32[8,768,1,3,128]{4,1,3,0,2:T(8,128)}, f32[8,768,1,128]{3,1,0,2:T(8,128)}, f32[8,768,1,128]{3,1,0,2:T(8,128)}) conditional(s32[]{:T(128)} %convert_element_type.124, (f32[8,768,1,3,128]{4,1,3,0,2:T(8,128)}, bf16[8,768,1,128]{3,1,0,2:T(8,128)(2,1)S(1)}, bf16[8,768,1,3,128]{4,1,3,0,2:T(8,128)(2,1)}, ...), branch_computations={%region_11.11_spmd, %region_12.12_spmd} | conditional | flops 9123790848 | bytes 234614944 | solution.py:99
  1403.5 84.6 %collective-permute-done.2 = bf16[8,768,1,128]{3,1,0,2:T(8,128)(2,1)S(1)} collective-permute-done((bf16[8,768,1,128]{3,1,0,2:T(8,128)(2,1)}, bf16[8,768,1,128]{3,1,0,2:T(8,128)(2,1)S(1)}, u32[]{:S(2)}, u32[]{:S(2)}) %collective-permute-start.2) | collective-permute-done | bytes 1572896 | tf_op jit(solution)/shard_map/while/body/eval_jaxpr/ppermute | solution.py:94
  1507.6 77.8 %conditional.5 = (f32[8,768,1,3,128]{4,1,3,0,2:T(8,128)}, f32[8,768,1,128]{3,1,0,2:T(8,128)}, f32[8,768,1,128]{3,1,0,2:T(8,128)}) conditional(s32[]{:T(128)} %convert_element_type.124, (f32[8,768,1,3,128]{4,1,3,0,2:T(8,128)}, bf16[8,768,1,128]{3,1,0,2:T(8,128)(2,1)S(1)}, bf16[8,768,1,3,128]{4,1,3,0,2:T(8,128)(2,1)}, ...), branch_computations={%region_11.11_spmd, %region_12.12_spmd} | conditional | flops 9123790848 | bytes 234614944 | solution.py:99
  1588.1 84.6 %collective-permute-done.2 = bf16[8,768,1,128]{3,1,0,2:T(8,128)(2,1)S(1)} collective-permute-done((bf16[8,768,1,128]{3,1,0,2:T(8,128)(2,1)}, bf16[8,768,1,128]{3,1,0,2:T(8,128)(2,1)S(1)}, u32[]{:S(2)}, u32[]{:S(2)}) %collective-permute-start.2) | collective-permute-done | bytes 1572896 | tf_op jit(solution)/shard_map/while/body/eval_jaxpr/ppermute | solution.py:94
  1692.3 77.8 %conditional.5 = (f32[8,768,1,3,128]{4,1,3,0,2:T(8,128)}, f32[8,768,1,128]{3,1,0,2:T(8,128)}, f32[8,768,1,128]{3,1,0,2:T(8,128)}) conditional(s32[]{:T(128)} %convert_element_type.124, (f32[8,768,1,3,128]{4,1,3,0,2:T(8,128)}, bf16[8,768,1,128]{3,1,0,2:T(8,128)(2,1)S(1)}, bf16[8,768,1,3,128]{4,1,3,0,2:T(8,128)(2,1)}, ...), branch_computations={%region_11.11_spmd, %region_12.12_spmd} | conditional | flops 9123790848 | bytes 234614944 | solution.py:99
  1772.8 84.6 %collective-permute-done.2 = bf16[8,768,1,128]{3,1,0,2:T(8,128)(2,1)S(1)} collective-permute-done((bf16[8,768,1,128]{3,1,0,2:T(8,128)(2,1)}, bf16[8,768,1,128]{3,1,0,2:T(8,128)(2,1)S(1)}, u32[]{:S(2)}, u32[]{:S(2)}) %collective-permute-start.2) | collective-permute-done | bytes 1572896 | tf_op jit(solution)/shard_map/while/body/eval_jaxpr/ppermute | solution.py:94
  1876.9 77.8 %conditional.5 = (f32[8,768,1,3,128]{4,1,3,0,2:T(8,128)}, f32[8,768,1,128]{3,1,0,2:T(8,128)}, f32[8,768,1,128]{3,1,0,2:T(8,128)}) conditional(s32[]{:T(128)} %convert_element_type.124, (f32[8,768,1,3,128]{4,1,3,0,2:T(8,128)}, bf16[8,768,1,128]{3,1,0,2:T(8,128)(2,1)S(1)}, bf16[8,768,1,3,128]{4,1,3,0,2:T(8,128)(2,1)}, ...), branch_computations={%region_11.11_spmd, %region_12.12_spmd} | conditional | flops 9123790848 | bytes 234614944 | solution.py:99
  1957.4 84.6 %collective-permute-done.2 = bf16[8,768,1,128]{3,1,0,2:T(8,128)(2,1)S(1)} collective-permute-done((bf16[8,768,1,128]{3,1,0,2:T(8,128)(2,1)}, bf16[8,768,1,128]{3,1,0,2:T(8,128)(2,1)S(1)}, u32[]{:S(2)}, u32[]{:S(2)}) %collective-permute-start.2) | collective-permute-done | bytes 1572896 | tf_op jit(solution)/shard_map/while/body/eval_jaxpr/ppermute | solution.py:94
  2061.6 77.8 %conditional.5 = (f32[8,768,1,3,128]{4,1,3,0,2:T(8,128)}, f32[8,768,1,128]{3,1,0,2:T(8,128)}, f32[8,768,1,128]{3,1,0,2:T(8,128)}) conditional(s32[]{:T(128)} %convert_element_type.124, (f32[8,768,1,3,128]{4,1,3,0,2:T(8,128)}, bf16[8,768,1,128]{3,1,0,2:T(8,128)(2,1)S(1)}, bf16[8,768,1,3,128]{4,1,3,0,2:T(8,128)(2,1)}, ...), branch_computations={%region_11.11_spmd, %region_12.12_spmd} | conditional | flops 9123790848 | bytes 234614944 | solution.py:99
  (400 shorter events, 1563.1 us)
Async XLA Ops:
  852.9 106.9 %collective-permute-start.4 = (f32[8,768,1,128]{3,1,0,2:T(8,128)}, f32[8,768,1,128]{3,1,0,2:T(8,128)}, u32[]{:S(2)}, u32[]{:S(2)}) collective-permute-start(f32[8,768,1,128]{3,1,0,2:T(8,128)} %get-tuple-element.876), channel_id=1, source_target_pairs={{0,1},{1,2},{2,3},{3,4},{4,5},{5,6},{6,7},{7,0},{8,9},{9,10},{10,1... | collective-permute-start | bytes 9437192 | tf_op jit(solution)/shard_map/while/body/eval_jaxpr/ppermute | solution.py:96
  855.5 104.3 %collective-permute-start.5 = (f32[8,768,1,128]{3,1,0,2:T(8,128)}, f32[8,768,1,128]{3,1,0,2:T(8,128)}, u32[]{:S(2)}, u32[]{:S(2)}) collective-permute-start(f32[8,768,1,128]{3,1,0,2:T(8,128)} %get-tuple-element.877), channel_id=1, source_target_pairs={{0,1},{1,2},{2,3},{3,4},{4,5},{5,6},{6,7},{7,0},{8,9},{9,10},{10,1... | collective-permute-start | bytes 9437192 | tf_op jit(solution)/shard_map/while/body/eval_jaxpr/ppermute | solution.py:97
  855.6 101.5 %collective-permute-start.3 = (bf16[8,768,1,128]{3,1,0,2:T(8,128)(2,1)}, bf16[8,768,1,128]{3,1,0,2:T(8,128)(2,1)}, u32[]{:S(2)}, u32[]{:S(2)}) collective-permute-start(bf16[8,768,1,128]{3,1,0,2:T(8,128)(2,1)} %get-tuple-element.879), channel_id=1, source_target_pairs={{0,1},{1,2},{2,3},{3,4},{4,5},{5,6},{6,7},{7,0},{8,9},{9,10},{10,1... | collective-permute-start | bytes 4718600 | tf_op jit(solution)/shard_map/while/body/eval_jaxpr/ppermute | solution.py:95
  1034.0 106.8 %collective-permute-start.4 = (f32[8,768,1,128]{3,1,0,2:T(8,128)}, f32[8,768,1,128]{3,1,0,2:T(8,128)}, u32[]{:S(2)}, u32[]{:S(2)}) collective-permute-start(f32[8,768,1,128]{3,1,0,2:T(8,128)} %get-tuple-element.876), channel_id=1, source_target_pairs={{0,1},{1,2},{2,3},{3,4},{4,5},{5,6},{6,7},{7,0},{8,9},{9,10},{10,1... | collective-permute-start | bytes 9437192 | tf_op jit(solution)/shard_map/while/body/eval_jaxpr/ppermute | solution.py:96
  1036.5 104.3 %collective-permute-start.5 = (f32[8,768,1,128]{3,1,0,2:T(8,128)}, f32[8,768,1,128]{3,1,0,2:T(8,128)}, u32[]{:S(2)}, u32[]{:S(2)}) collective-permute-start(f32[8,768,1,128]{3,1,0,2:T(8,128)} %get-tuple-element.877), channel_id=1, source_target_pairs={{0,1},{1,2},{2,3},{3,4},{4,5},{5,6},{6,7},{7,0},{8,9},{9,10},{10,1... | collective-permute-start | bytes 9437192 | tf_op jit(solution)/shard_map/while/body/eval_jaxpr/ppermute | solution.py:97
  1036.6 84.7 %collective-permute-start.2 = (bf16[8,768,1,128]{3,1,0,2:T(8,128)(2,1)}, bf16[8,768,1,128]{3,1,0,2:T(8,128)(2,1)S(1)}, u32[]{:S(2)}, u32[]{:S(2)}) collective-permute-start(bf16[8,768,1,128]{3,1,0,2:T(8,128)(2,1)} %get-tuple-element.878), channel_id=1, source_target_pairs={{0,1},{1,2},{2,3},{3,4},{4,5},{5,6},{6,7},{7,0},{8,9},{9,10},{10,1... | collective-permute-start | bytes 4718600 | tf_op jit(solution)/shard_map/while/body/eval_jaxpr/ppermute | solution.py:94
  1036.6 101.5 %collective-permute-start.3 = (bf16[8,768,1,128]{3,1,0,2:T(8,128)(2,1)}, bf16[8,768,1,128]{3,1,0,2:T(8,128)(2,1)}, u32[]{:S(2)}, u32[]{:S(2)}) collective-permute-start(bf16[8,768,1,128]{3,1,0,2:T(8,128)(2,1)} %get-tuple-element.879), channel_id=1, source_target_pairs={{0,1},{1,2},{2,3},{3,4},{4,5},{5,6},{6,7},{7,0},{8,9},{9,10},{10,1... | collective-permute-start | bytes 4718600 | tf_op jit(solution)/shard_map/while/body/eval_jaxpr/ppermute | solution.py:95
  1218.7 104.3 %collective-permute-start.4 = (f32[8,768,1,128]{3,1,0,2:T(8,128)}, f32[8,768,1,128]{3,1,0,2:T(8,128)}, u32[]{:S(2)}, u32[]{:S(2)}) collective-permute-start(f32[8,768,1,128]{3,1,0,2:T(8,128)} %get-tuple-element.876), channel_id=1, source_target_pairs={{0,1},{1,2},{2,3},{3,4},{4,5},{5,6},{6,7},{7,0},{8,9},{9,10},{10,1... | collective-permute-start | bytes 9437192 | tf_op jit(solution)/shard_map/while/body/eval_jaxpr/ppermute | solution.py:96
  1218.7 104.3 %collective-permute-start.5 = (f32[8,768,1,128]{3,1,0,2:T(8,128)}, f32[8,768,1,128]{3,1,0,2:T(8,128)}, u32[]{:S(2)}, u32[]{:S(2)}) collective-permute-start(f32[8,768,1,128]{3,1,0,2:T(8,128)} %get-tuple-element.877), channel_id=1, source_target_pairs={{0,1},{1,2},{2,3},{3,4},{4,5},{5,6},{6,7},{7,0},{8,9},{9,10},{10,1... | collective-permute-start | bytes 9437192 | tf_op jit(solution)/shard_map/while/body/eval_jaxpr/ppermute | solution.py:97
  1218.8 101.5 %collective-permute-start.3 = (bf16[8,768,1,128]{3,1,0,2:T(8,128)(2,1)}, bf16[8,768,1,128]{3,1,0,2:T(8,128)(2,1)}, u32[]{:S(2)}, u32[]{:S(2)}) collective-permute-start(bf16[8,768,1,128]{3,1,0,2:T(8,128)(2,1)} %get-tuple-element.879), channel_id=1, source_target_pairs={{0,1},{1,2},{2,3},{3,4},{4,5},{5,6},{6,7},{7,0},{8,9},{9,10},{10,1... | collective-permute-start | bytes 4718600 | tf_op jit(solution)/shard_map/while/body/eval_jaxpr/ppermute | solution.py:95
  1400.8 106.8 %collective-permute-start.4 = (f32[8,768,1,128]{3,1,0,2:T(8,128)}, f32[8,768,1,128]{3,1,0,2:T(8,128)}, u32[]{:S(2)}, u32[]{:S(2)}) collective-permute-start(f32[8,768,1,128]{3,1,0,2:T(8,128)} %get-tuple-element.876), channel_id=1, source_target_pairs={{0,1},{1,2},{2,3},{3,4},{4,5},{5,6},{6,7},{7,0},{8,9},{9,10},{10,1... | collective-permute-start | bytes 9437192 | tf_op jit(solution)/shard_map/while/body/eval_jaxpr/ppermute | solution.py:96
  1403.3 104.3 %collective-permute-start.5 = (f32[8,768,1,128]{3,1,0,2:T(8,128)}, f32[8,768,1,128]{3,1,0,2:T(8,128)}, u32[]{:S(2)}, u32[]{:S(2)}) collective-permute-start(f32[8,768,1,128]{3,1,0,2:T(8,128)} %get-tuple-element.877), channel_id=1, source_target_pairs={{0,1},{1,2},{2,3},{3,4},{4,5},{5,6},{6,7},{7,0},{8,9},{9,10},{10,1... | collective-permute-start | bytes 9437192 | tf_op jit(solution)/shard_map/while/body/eval_jaxpr/ppermute | solution.py:97
  1403.3 84.7 %collective-permute-start.2 = (bf16[8,768,1,128]{3,1,0,2:T(8,128)(2,1)}, bf16[8,768,1,128]{3,1,0,2:T(8,128)(2,1)S(1)}, u32[]{:S(2)}, u32[]{:S(2)}) collective-permute-start(bf16[8,768,1,128]{3,1,0,2:T(8,128)(2,1)} %get-tuple-element.878), channel_id=1, source_target_pairs={{0,1},{1,2},{2,3},{3,4},{4,5},{5,6},{6,7},{7,0},{8,9},{9,10},{10,1... | collective-permute-start | bytes 4718600 | tf_op jit(solution)/shard_map/while/body/eval_jaxpr/ppermute | solution.py:94
  1403.4 101.5 %collective-permute-start.3 = (bf16[8,768,1,128]{3,1,0,2:T(8,128)(2,1)}, bf16[8,768,1,128]{3,1,0,2:T(8,128)(2,1)}, u32[]{:S(2)}, u32[]{:S(2)}) collective-permute-start(bf16[8,768,1,128]{3,1,0,2:T(8,128)(2,1)} %get-tuple-element.879), channel_id=1, source_target_pairs={{0,1},{1,2},{2,3},{3,4},{4,5},{5,6},{6,7},{7,0},{8,9},{9,10},{10,1... | collective-permute-start | bytes 4718600 | tf_op jit(solution)/shard_map/while/body/eval_jaxpr/ppermute | solution.py:95
  1585.5 106.8 %collective-permute-start.4 = (f32[8,768,1,128]{3,1,0,2:T(8,128)}, f32[8,768,1,128]{3,1,0,2:T(8,128)}, u32[]{:S(2)}, u32[]{:S(2)}) collective-permute-start(f32[8,768,1,128]{3,1,0,2:T(8,128)} %get-tuple-element.876), channel_id=1, source_target_pairs={{0,1},{1,2},{2,3},{3,4},{4,5},{5,6},{6,7},{7,0},{8,9},{9,10},{10,1... | collective-permute-start | bytes 9437192 | tf_op jit(solution)/shard_map/while/body/eval_jaxpr/ppermute | solution.py:96
  1588.0 104.3 %collective-permute-start.5 = (f32[8,768,1,128]{3,1,0,2:T(8,128)}, f32[8,768,1,128]{3,1,0,2:T(8,128)}, u32[]{:S(2)}, u32[]{:S(2)}) collective-permute-start(f32[8,768,1,128]{3,1,0,2:T(8,128)} %get-tuple-element.877), channel_id=1, source_target_pairs={{0,1},{1,2},{2,3},{3,4},{4,5},{5,6},{6,7},{7,0},{8,9},{9,10},{10,1... | collective-permute-start | bytes 9437192 | tf_op jit(solution)/shard_map/while/body/eval_jaxpr/ppermute | solution.py:97
  1588.0 101.5 %collective-permute-start.3 = (bf16[8,768,1,128]{3,1,0,2:T(8,128)(2,1)}, bf16[8,768,1,128]{3,1,0,2:T(8,128)(2,1)}, u32[]{:S(2)}, u32[]{:S(2)}) collective-permute-start(bf16[8,768,1,128]{3,1,0,2:T(8,128)(2,1)} %get-tuple-element.879), channel_id=1, source_target_pairs={{0,1},{1,2},{2,3},{3,4},{4,5},{5,6},{6,7},{7,0},{8,9},{9,10},{10,1... | collective-permute-start | bytes 4718600 | tf_op jit(solution)/shard_map/while/body/eval_jaxpr/ppermute | solution.py:95
  1770.1 106.9 %collective-permute-start.4 = (f32[8,768,1,128]{3,1,0,2:T(8,128)}, f32[8,768,1,128]{3,1,0,2:T(8,128)}, u32[]{:S(2)}, u32[]{:S(2)}) collective-permute-start(f32[8,768,1,128]{3,1,0,2:T(8,128)} %get-tuple-element.876), channel_id=1, source_target_pairs={{0,1},{1,2},{2,3},{3,4},{4,5},{5,6},{6,7},{7,0},{8,9},{9,10},{10,1... | collective-permute-start | bytes 9437192 | tf_op jit(solution)/shard_map/while/body/eval_jaxpr/ppermute | solution.py:96
  1772.6 104.3 %collective-permute-start.5 = (f32[8,768,1,128]{3,1,0,2:T(8,128)}, f32[8,768,1,128]{3,1,0,2:T(8,128)}, u32[]{:S(2)}, u32[]{:S(2)}) collective-permute-start(f32[8,768,1,128]{3,1,0,2:T(8,128)} %get-tuple-element.877), channel_id=1, source_target_pairs={{0,1},{1,2},{2,3},{3,4},{4,5},{5,6},{6,7},{7,0},{8,9},{9,10},{10,1... | collective-permute-start | bytes 9437192 | tf_op jit(solution)/shard_map/while/body/eval_jaxpr/ppermute | solution.py:97
  1772.6 84.7 %collective-permute-start.2 = (bf16[8,768,1,128]{3,1,0,2:T(8,128)(2,1)}, bf16[8,768,1,128]{3,1,0,2:T(8,128)(2,1)S(1)}, u32[]{:S(2)}, u32[]{:S(2)}) collective-permute-start(bf16[8,768,1,128]{3,1,0,2:T(8,128)(2,1)} %get-tuple-element.878), channel_id=1, source_target_pairs={{0,1},{1,2},{2,3},{3,4},{4,5},{5,6},{6,7},{7,0},{8,9},{9,10},{10,1... | collective-permute-start | bytes 4718600 | tf_op jit(solution)/shard_map/while/body/eval_jaxpr/ppermute | solution.py:94
  1772.7 101.5 %collective-permute-start.3 = (bf16[8,768,1,128]{3,1,0,2:T(8,128)(2,1)}, bf16[8,768,1,128]{3,1,0,2:T(8,128)(2,1)}, u32[]{:S(2)}, u32[]{:S(2)}) collective-permute-start(bf16[8,768,1,128]{3,1,0,2:T(8,128)(2,1)} %get-tuple-element.879), channel_id=1, source_target_pairs={{0,1},{1,2},{2,3},{3,4},{4,5},{5,6},{6,7},{7,0},{8,9},{9,10},{10,1... | collective-permute-start | bytes 4718600 | tf_op jit(solution)/shard_map/while/body/eval_jaxpr/ppermute | solution.py:95
  1954.8 106.8 %collective-permute-start.4 = (f32[8,768,1,128]{3,1,0,2:T(8,128)}, f32[8,768,1,128]{3,1,0,2:T(8,128)}, u32[]{:S(2)}, u32[]{:S(2)}) collective-permute-start(f32[8,768,1,128]{3,1,0,2:T(8,128)} %get-tuple-element.876), channel_id=1, source_target_pairs={{0,1},{1,2},{2,3},{3,4},{4,5},{5,6},{6,7},{7,0},{8,9},{9,10},{10,1... | collective-permute-start | bytes 9437192 | tf_op jit(solution)/shard_map/while/body/eval_jaxpr/ppermute | solution.py:96
  1957.3 104.3 %collective-permute-start.5 = (f32[8,768,1,128]{3,1,0,2:T(8,128)}, f32[8,768,1,128]{3,1,0,2:T(8,128)}, u32[]{:S(2)}, u32[]{:S(2)}) collective-permute-start(f32[8,768,1,128]{3,1,0,2:T(8,128)} %get-tuple-element.877), channel_id=1, source_target_pairs={{0,1},{1,2},{2,3},{3,4},{4,5},{5,6},{6,7},{7,0},{8,9},{9,10},{10,1... | collective-permute-start | bytes 9437192 | tf_op jit(solution)/shard_map/while/body/eval_jaxpr/ppermute | solution.py:97
  1957.3 101.5 %collective-permute-start.3 = (bf16[8,768,1,128]{3,1,0,2:T(8,128)(2,1)}, bf16[8,768,1,128]{3,1,0,2:T(8,128)(2,1)}, u32[]{:S(2)}, u32[]{:S(2)}) collective-permute-start(bf16[8,768,1,128]{3,1,0,2:T(8,128)(2,1)} %get-tuple-element.879), channel_id=1, source_target_pairs={{0,1},{1,2},{2,3},{3,4},{4,5},{5,6},{6,7},{7,0},{8,9},{9,10},{10,1... | collective-permute-start | bytes 4718600 | tf_op jit(solution)/shard_map/while/body/eval_jaxpr/ppermute | solution.py:95
  (86 other events, 2250.2 us)
where the time goes:
time: 2230 us; the launch traced here: 2190 us
  waiting for transfers between devices  969 us (43%)
  matrix products  829 us (37%)
  other arithmetic  230 us (10%)
  local copies, waits for them, and re-layouts  124 us (6%)
  starting transfers between devices  34.7 us (2%)
    ppermute x7, waiting for transfers between devices, bwd_step(): k_cur = lax.ppermute(k_cur, 'ctx', perm_next)  592 us
    dot_general x15, matrix products, scores_of(): jnp.einsum('bqhgd,bkhd->bhgqk', q_blk, k_blk, preferred_element_type=jnp....  224 us
    dot_general x8, matrix products, bwd_block(): jnp.einsum('bqhgd,bkhd->bhgqk', g_blk, v_blk, preferred_element_type=jnp....  165 us
    dot_general x8, matrix products, fwd_update(): jnp.einsum('bhgqk,bkhd->bhgqd', prob_tile.astype(jnp.bfloat16), v_blk, pr...  131 us
    dot_general x8, matrix products, bwd_block(): jnp.einsum('bhgqk,bqhgd->bkhd', prob_tile.astype(jnp.bfloat16), g_blk, pr...  127 us
    ppermute x7, waiting for transfers between devices, fwd_step(): k_cur = lax.ppermute(k_cur, 'ctx', perm_next)  124 us
    ppermute x7, waiting for transfers between devices, fwd_step(): v_cur = lax.ppermute(v_cur, 'ctx', perm_next)  115 us
    ppermute x7, waiting for transfers between devices, bwd_step(): v_cur = lax.ppermute(v_cur, 'ctx', perm_next)  110 us
  transfers between devices with their start and end apart: 44, of which 30 were waited for; matrix products, arithmetic and copies ran while one was open for 2% of the time, Pallas kernels for 0%

commit v1 on v0

v1 whole, which is shorter than its diff:
```python
import functools
import math

import jax
import jax.numpy as jnp
from jax import lax
from jax.experimental import pallas as pl
from jax.experimental.pallas import tpu as pltpu
from jax.sharding import PartitionSpec as P

f32=jnp.float32; bf16=jnp.bfloat16
NEG=-1e30
R=256
def rowcol(n):
    return lax.broadcasted_iota(jnp.int32,(n,n),0), lax.broadcasted_iota(jnp.int32,(n,n),1)

class Core:
    def __init__(s, seg, nseg, d):
        s.seg=seg; s.ns=nseg; s.d=d; s.nr=seg//R; s.c=(d**-0.5)*math.log2(math.e)
    def at(s, i, r=None):
        if r is None: return pl.ds(pl.multiple_of(i*s.seg, s.seg), s.seg)
        return pl.ds(pl.multiple_of(i*s.seg+r*R, R), R)
    def fa(s, kb, qT, sb, mb, qi, ki, diag, r, c, m):
        cs=slice(r*R,(r+1)*R); rs=slice(c*R,(c+1)*R)
        if diag and c>r: return m
        x=jnp.dot(kb[s.at(ki,c),:], qT[:, s.at(qi,r)], preferred_element_type=f32)
        if diag and c==r:
            ri,ci=rowcol(R)
            x=jnp.where(ri<=ci, x, NEG)
        sb[rs,cs]=x
        x=jnp.max(x,axis=0,keepdims=True)
        m=x if m is None else jnp.maximum(m,x)
        if c==(r if diag else s.nr-1): mb[:,cs]=m
        return m
    def fb(s, vT, sb, mb, acc, ms, ls, sel, ki, diag, r, c, cx):
        cs=slice(r*R,(r+1)*R); rs=slice(c*R,(c+1)*R)
        if diag and c>r: return cx
        if c==0:
            mn=mb[:,cs]*s.c
            if not diag: mn=jnp.maximum(ms[sel,:,cs],mn)
        else: mn,l0,o0=cx
        p=jnp.exp2(sb[rs,cs]*s.c-mn)
        l=jnp.sum(p,axis=0,keepdims=True)
        o=jnp.dot(vT[:,s.at(ki,c)], p.astype(bf16), preferred_element_type=f32)
        if c: l=l0+l; o=o0+o
        if c==(r if diag else s.nr-1):
            if not diag:
                al=jnp.exp2(ms[sel,:,cs]-mn)
                l=l+ls[sel,:,cs]*al
                o=o+acc[sel,:,cs]*al
            ms[sel,:,cs]=mn; ls[sel,:,cs]=l; acc[sel,:,cs]=o
        return mn,l,o
    def ba(s, q, do, kT, vT, lsc, dsc, bufs, qi, sel, ki, diag, r):
        pb,db,tb=bufs
        rs=slice(r*R,(r+1)*R)
        n=(r+1)*R if diag else s.seg
        ks=pl.ds(pl.multiple_of(ki*s.seg,s.seg),n)
        x=jnp.dot(q[s.at(qi,r),:], kT[:,ks], preferred_element_type=f32)
        dp=jnp.dot(do[s.at(qi,r),:], vT[:,ks], preferred_element_type=f32)
        l=jnp.concatenate([lsc[sel,rs,:]]*(n//128),axis=1)
        dd=jnp.concatenate([dsc[sel,rs,:]]*(n//128),axis=1)
        p=jnp.exp2(x*s.c-l)
        if diag:
            ri,ci=rowcol(R)
            t=jnp.where(ri>=ci,p[:,r*R:],0.0)
            p=jnp.concatenate([p[:,:r*R],t],axis=1) if r else t
        ds=(p*(dp-dd)).astype(bf16)
        pb[rs,:n]=p.astype(bf16); db[rs,:n]=ds
        tb[:n,rs]=ds.T
    def bb(s, qT, doT, kT, dqT, dkT, dvT, bufs, qi, sel, ki, diag, r, cx):
        pb,db,tb=bufs
        rs=slice(r*R,(r+1)*R)
        n=(r+1)*R if diag else s.seg
        ks=pl.ds(pl.multiple_of(ki*s.seg,s.seg),n)
        dot=lambda a,b: jnp.dot(a,b,preferred_element_type=f32)
        x=dot(doT[:,s.at(qi,r)], pb[rs,:n])
        y=dot(qT[:,s.at(qi,r)], db[rs,:n])
        z=dot(kT[:,ks], tb[:n,rs])
        cols=slice(r*R,(r+1)*R)
        if diag:
            dqT[sel,:,cols]=z
            dvT[:,ks]+=x; dkT[:,ks]+=y
            return None
        dqT[sel,:,cols]+=z
        x,y=(x,y) if cx is None else (cx[0]+x,cx[1]+y)
        if r==s.nr-1:
            dvT[:,ks]+=x; dkT[:,ks]+=y
        return x,y
    def steps(s, y):
        a=y; b=s.ns-1-y
        out=[(0,a,a,True),(1,b,b,True)]
        for t in range(s.ns-1):
            early = t<y
            out.append((jnp.where(early,0,1), jnp.where(early,a,b), jnp.where(early,t,t-y), False))
        return out
    def forward(s, y, kb, vT, qT, oT, lse, sbs, mbs, acc, ms, ls):
        st=s.steps(y)
        def A(t,r,c,m): sel,qi,ki,dg=st[t]; return s.fa(kb,qT,sbs[t%2],mbs[t%2],qi,ki,dg,r,c,m)
        def B(t,r,c,cx): sel,qi,ki,dg=st[t]; return s.fb(vT,sbs[t%2],mbs[t%2],acc,ms,ls,sel,ki,dg,r,c,cx)
        for r in range(s.nr):
            m=None
            for c in range(s.nr): m=A(0,r,c,m)
        for t in range(len(st)):
            for r in range(s.nr):
                m=cx=None
                for c in range(s.nr):
                    if t+1<len(st): m=A(t+1,r,c,m)
                    cx=B(t,r,c,cx)
        for sel,i in ((0,y),(1,s.ns-1-y)):
            l=ls[sel]
            oT[:,s.at(i)]=(acc[sel]*(1.0/l)).astype(bf16)
            lse[i]=ms[sel]+jnp.log2(l)
    def backward(s, y, q, do, qT, doT, kT, vT, oT, lse, lsc, dsc, dqT, dkT, dvT, bufs):
        for sel,i in ((0,y),(1,s.ns-1-y)):
            drow=jnp.sum(doT[:,s.at(i)].astype(f32)*oT[:,s.at(i)].astype(f32),axis=0,keepdims=True)
            lsc[sel]=jnp.broadcast_to(lse[i],(128,s.seg)).T
            dsc[sel]=jnp.broadcast_to(drow,(128,s.seg)).T
        st=s.steps(y)
        def A(t,r): sel,qi,ki,dg=st[t]; s.ba(q,do,kT,vT,lsc,dsc,bufs[t%2],qi,sel,ki,dg,r)
        def B(t,r,cx): sel,qi,ki,dg=st[t]; return s.bb(qT,doT,kT,dqT,dkT,dvT,bufs[t%2],qi,sel,ki,dg,r,cx)
        for r in range(s.nr): A(0,r)
        for t in range(len(st)):
            cx=None
            for r in range(s.nr):
                if t+1<len(st): A(t+1,r)
                cx=B(t,r,cx)


MESH = pl.DeviceIdType.MESH


def kernel(n, qh, doh, kh, vh, oo, dqo, dko, dvo, q, do, ob, k, v, kT, vT, qT, doT, oT, lse, acc, ms, ls, lsc, dsc, dqT, dkT, dvT,
           s0, s1, m0, m1, p0, p1, d0, d1, t0, t1, insem, outsem, rk, rv, rq, rdo, ro, rdq, rdk, rdv):
    heads, shard, dim = qh.shape[1:]
    half = shard // 2
    segs = n
    core = Core(shard, segs, dim)
    me = lax.axis_index("ctx")
    scale = dim ** -0.5

    barrier = pltpu.get_barrier_semaphore()
    for off in range(1, n):
        pl.semaphore_signal(barrier, inc=1, device_id={"ctx": lax.rem(me + off, n)}, device_id_type=MESH)
    pl.semaphore_wait(barrier, n - 1)

    def rows(piece):
        return pl.ds(pl.multiple_of(piece * half, half), half)

    def own(part):
        return pl.ds(part * half, half)

    def piece(dev, part):
        return dev if part == 0 else 2 * n - 1 - dev

    def spread(src, dst, sem):
        for part in (0, 1):
            pltpu.make_async_copy(src(me, part), dst(part), sem).start()

        def send(off, _):
            dev = lax.rem(me + off, n)
            for part in (0, 1):
                pltpu.make_async_remote_copy(src(dev, part), dst(part), insem.at[dev], sem, device_id={"ctx": dev}, device_id_type=MESH).start()
            return 0

        lax.fori_loop(1, n, send, 0)

    def gather(src, dst, sem):
        for part in (0, 1):
            pltpu.make_async_copy(src(me, part), dst(part), sem).start()

        def send(off, _):
            dev = lax.rem(me + off, n)
            for part in (0, 1):
                pltpu.make_async_remote_copy(src(dev, part), dst(part), outsem.at[dev], sem, device_id={"ctx": dev}, device_id_type=MESH).start()
            return 0

        lax.fori_loop(1, n, send, 0)

    def arrived(ref, sem):
        pltpu.make_async_remote_copy(ref, ref, insem.at[me], sem, device_id={"ctx": lax.rem(me + 1, n)}, device_id_type=MESH).wait_recv()

    def sent(sem):
        pltpu.make_async_remote_copy(kh, kh, sem, rk, device_id={"ctx": lax.rem(me + 1, n)}, device_id_type=MESH).wait_send()

    spread(lambda dev, part: kh.at[dev, own(part)], lambda part: k.at[rows(piece(me, part))], rk)
    spread(lambda dev, part: vh.at[dev, own(part)], lambda part: v.at[rows(piece(me, part))], rv)
    for h in range(heads):
        spread(lambda dev, part: qh.at[dev, h, own(part)], lambda part: q.at[h, rows(piece(me, part))], rq.at[h])
        spread(lambda dev, part: doh.at[dev, h, own(part)], lambda part: do.at[h, rows(piece(me, part))], rdo.at[h])

    def turn(src, dst):
        def body(i, _):
            dst[:, core.at(i)] = src[core.at(i), :].T
            return 0

        lax.fori_loop(0, segs, body, 0)

    dkT[...] = jnp.zeros_like(dkT)
    dvT[...] = jnp.zeros_like(dvT)
    arrived(k, rk)
    turn(k, kT)
    arrived(v, rv)
    turn(v, vT)

    def head(h, _):
        arrived(q.at[h], rq.at[h])
        turn(q.at[h], qT)

        def fwd(y, _):
            core.forward(y, k, vT, qT, oT, lse, (s0, s1), (m0, m1), acc, ms, ls)
            for i in (y, segs - 1 - y):
                ob[h, core.at(i), :] = oT[:, core.at(i)].T
            return 0

        lax.fori_loop(0, segs // 2, fwd, 0)
        arrived(do.at[h], rdo.at[h])
        turn(do.at[h], doT)
        gather(lambda dev, part: ob.at[h, rows(piece(dev, part))], lambda part: oo.at[me, h, own(part)], ro)

        def bwd(y, _):
            core.backward(y, q.at[h], do.at[h], qT, doT, kT, vT, oT, lse, lsc, dsc, dqT, dkT, dvT, ((p0, d0, t0), (p1, d1, t1)))
            for sel, i in ((0, y), (1, segs - 1 - y)):
                q[h, core.at(i), :] = (dqT[sel] * scale).astype(bf16).T
            return 0

        lax.fori_loop(0, segs // 2, bwd, 0)
        gather(lambda dev, part: q.at[h, rows(piece(dev, part))], lambda part: dqo.at[me, h, own(part)], rdq)
        return 0

    lax.fori_loop(0, heads, head, 0)

    def finish(i, _):
        k[core.at(i), :] = (dkT[:, core.at(i)] * scale).astype(bf16).T
        v[core.at(i), :] = dvT[:, core.at(i)].astype(bf16).T
        return 0

    lax.fori_loop(0, segs, finish, 0)
    gather(lambda dev, part: k.at[rows(piece(dev, part))], lambda part: dko.at[me, own(part)], rdk)
    gather(lambda dev, part: v.at[rows(piece(dev, part))], lambda part: dvo.at[me, own(part)], rdv)
    for off in range(1, n):
        sent(insem.at[lax.rem(me + off, n)])
        sent(outsem.at[lax.rem(me + off, n)])
    arrived(oo, ro)
    arrived(dqo, rdq)
    arrived(dko, rdk)
    arrived(dvo, rdv)


def solution(mesh):
    n = mesh.shape["ctx"]
    spec = P("data", "ctx", None, None)

    def local(queries, keys_in, values_in, grad_out):
        batch, shard, heads, dim = queries.shape
        assert batch == n and keys_in.shape[2] == 1
        seq = n * shard
        q, g = (t.transpose(0, 2, 1, 3) for t in (queries, grad_out))
        k, v = (t.reshape(batch, shard, dim) for t in (keys_in, values_in))
        hbm = pl.BlockSpec(memory_space=pl.ANY)
        vm, dma = pltpu.VMEM, pltpu.SemaphoreType.DMA
        wide = jax.ShapeDtypeStruct(q.shape, bf16)
        thin = jax.ShapeDtypeStruct(k.shape, bf16)
        o, dq, dk, dv = pl.pallas_call(
            functools.partial(kernel, n),
            out_shape=[wide, wide, thin, thin],
            in_specs=[hbm] * 4,
            out_specs=[hbm] * 4,
            scratch_shapes=[vm((heads, seq, dim), bf16)] * 3 + [vm((seq, dim), bf16)] * 2 + [vm((dim, seq), bf16)] * 5
            + [vm((n, 1, shard), f32), vm((2, dim, shard), f32), vm((2, 1, shard), f32), vm((2, 1, shard), f32)]
            + [vm((2, shard, 128), f32)] * 2 + [vm((2, dim, shard), f32)] + [vm((dim, seq), f32)] * 2
            + [vm((shard, shard), f32)] * 2 + [vm((1, shard), f32)] * 2 + [vm((shard, shard), bf16)] * 6
            + [dma((n,)), dma((n,)), dma, dma, dma((heads,)), dma((heads,)), dma, dma, dma, dma],
            compiler_params=pltpu.CompilerParams(collective_id=0, has_side_effects=True, vmem_limit_bytes=67043328),
            name="attention",
        )(q, g, k, v)
        o, dq = (t.transpose(0, 2, 1, 3) for t in (o, dq))
        dk, dv = (t.reshape(keys_in.shape) for t in (dk, dv))
        return o, dq, dk, dv

    return jax.shard_map(local, mesh=mesh, in_specs=(spec,) * 4, out_specs=(spec,) * 4, check_vma=False)
```

time: 2230 us -> 363 us (0.16); the launches traced: 2190 us -> 363 us
  waiting for transfers between devices: 969 us -> 0 us
  matrix products: 829 us -> 0 us
  Pallas kernels: 0 us -> 353 us
  other arithmetic: 230 us -> 0 us
  local copies, waits for them, and re-layouts: 124 us -> 10.1 us
  starting transfers between devices: 34.7 us -> 0 us
    ppermute x44 -> x0, waiting for transfers between devices: 969 us -> none  [the longest x7 592 us: bwd_step(): k_cur = lax.ppermute(k_cur, 'ctx', perm_next)]
    dot_general x55 -> x0, matrix products: 829 us -> none  [the longest x15 224 us: scores_of(): jnp.einsum('bqhgd,bkhd->bhgqk', q_blk, k_blk, preferred_element_type=jnp....]
    pallas_call x0 -> x1, Pallas kernels: none -> 353 us  [local(): pl.pallas_call(functools.partial(kernel, n), out_shape=[wide, wide, thin,...]
    reduce_sum x8 -> x0, other arithmetic: 105 us -> none  [fwd_update(): new_sum = run_sum * decay_factor + jnp.sum(prob_tile, axis=-1)]
    concatenate x19 -> x0, other arithmetic: 99 us -> none  [the longest x12 54.2 us: fwd_future(): jnp.concatenate([low_part, high_part], axis=3)]
    while x35 -> x0, local copies, waits for them, and re-layouts: 70.5 us -> none
    slice x14 -> x0, local copies, waits for them, and re-layouts: 36.5 us -> none  [the longest x6 17.6 us: bwd_future(): dq_acc[:, :half_len]]
    ppermute x44 -> x0, starting transfers between devices: 34.7 us -> none  [the longest x7 15.2 us: fwd_step(): k_cur = lax.ppermute(k_cur, 'ctx', perm_next)]
  transfers between devices with their start and end apart: 44 -> 0, of which waited for: 30 -> 0; matrix products, arithmetic and copies ran while one was open for 2% -> 0% of each run, Pallas kernels for 0% -> 0%
where the time goes in v1:
time: 363 us
  Pallas kernels  353 us (97%)
  local copies, waits for them, and re-layouts  10.1 us (3%)
    pallas_call x1, Pallas kernels, local(): pl.pallas_call(functools.partial(kernel, n), out_shape=[wide, wide, thin,...  353 us
    unnamed x10, local copies, waits for them, and re-layouts  10.1 us

profile of v1, /device:TPU:81, one launch (start us, length us, event | category | flops | bytes accessed | tf_op | source)
XLA Modules:
  0.0 363.3 jit_solution(1610832798848168407)
XLA Ops:
  0.6 352.6 %attention.1 = (bf16[8,3,768,128]{3,2,1,0:T(8,128)(2,1)}, bf16[8,3,768,128]{3,2,1,0:T(8,128)(2,1)}, bf16[8,768,128]{2,1,0:T(8,128)(2,1)}, bf16[8,768,128]{2,1,0:T(8,128)(2,1)}) custom-call(bf16[8,3,768,128]{3,2,1,0:T(8,128)(2,1)} %bitcast.12, bf16[8,3,768,128]{3,2,1,0:T(8,128)(2,1)} %bitcast.13, bf16[8,768,128]{2,1,0:T(8,128)(2,1)} %bitcast.16, ...), custom_call_target="tpu_custom_call" | custom-call | tf_op jit(solution)/shard_map/attention/pallas_call | solution.py:263
  353.3 0.0 copy-start
  353.3 5.1 %copy.14 = bf16[8,768,3,128]{3,1,2,0:T(8,128)(2,1)} copy(bf16[8,768,3,128]{3,1,2,0:T(8,128)(2,1)} %bitcast.15) | data formatting | bytes 9437184
  358.4 0.0 copy-done
  358.4 0.0 copy-start.2
  358.4 0.0 copy-start.1
  358.4 2.4 copy.15
  360.8 0.1 copy-done.2
  360.9 1.1 copy.16
  362.1 0.1 copy-done.1
  362.2 1.1 copy.17
Async XLA Ops:
  353.3 5.1 %copy-start = (bf16[8,3,768,128]{3,2,1,0:T(8,128)(2,1)S(1)}, bf16[8,3,768,128]{3,2,1,0:T(8,128)(2,1)}, u32[]{:S(2)}) copy-start(bf16[8,3,768,128]{3,2,1,0:T(8,128)(2,1)} %get-tuple-element.9) | copy-start | bytes 14155780
  358.4 2.5 copy-start.2
  358.4 3.8 %copy-start.1 = (bf16[8,768,128]{2,1,0:T(8,128)(2,1)S(1)}, bf16[8,768,128]{2,1,0:T(8,128)(2,1)}, u32[]{:S(2)}) copy-start(bf16[8,768,128]{2,1,0:T(8,128)(2,1)} %get-tuple-element.11) | copy-start | bytes 4718596

commit v2 on v0

v2 whole, which is shorter than its diff:
```python
import functools
import math

import jax
import jax.numpy as jnp
from jax import lax
from jax.experimental import pallas as pl
from jax.experimental.pallas import tpu as pltpu
from jax.sharding import PartitionSpec as P

MESH = pl.DeviceIdType.MESH
f32, bf16 = jnp.float32, jnp.bfloat16
NEG = -1e30
R = 256


def dot(a, b):
    return jnp.dot(a, b, preferred_element_type=f32)


def triangle(flip):
    i, j = lax.broadcasted_iota(jnp.int32, (R, R), 0), lax.broadcasted_iota(jnp.int32, (R, R), 1)
    return i <= j if flip else i >= j


def kernel(n, qh, doh, kh, vh, oo, dqo, dko, dvo, q, do, ob, k, v, kT, vT, qT, doT, oT, acc, ms, ls, lsc, dsc, dkT, dvT,
           sb0, sb1, sb2, mb0, mb1, mb2, pb0, pb1, pb2, db0, db1, db2, tb0, tb1, tb2, insem, outsem, rk, rv, rq, rdo, ro, rdq, rdk, rdv):
    heads, shard, dim = qh.shape[1:]
    half, seg, segs, chips = shard // 2, shard, n, n // 2
    nr = seg // R
    sbs, mbs, bufs = (sb0, sb1, sb2), (mb0, mb1, mb2), ((pb0, db0, tb0), (pb1, db1, tb1), (pb2, db2, tb2))
    me = lax.axis_index("ctx")
    chip = me // 2
    scale = dim ** -0.5
    c2 = scale * math.log2(math.e)

    barrier = pltpu.get_barrier_semaphore()
    for off in range(1, n):
        pl.semaphore_signal(barrier, inc=1, device_id={"ctx": lax.rem(me + off, n)}, device_id_type=MESH)
    pl.semaphore_wait(barrier, n - 1)

    def rows(piece):
        return pl.ds(pl.multiple_of(piece * half, half), half)

    def at(i, r=None, m=1):
        if r is None:
            return pl.ds(pl.multiple_of(i * seg, seg), seg)
        return pl.ds(pl.multiple_of(i * seg + r * R, R), m * R)

    def to(dev, src, dst, sends, recvs):
        pltpu.make_async_remote_copy(src, dst, sends.at[dev], recvs, device_id={"ctx": dev}, device_id_type=MESH).start()

    def arrived(ref, sem):
        pltpu.make_async_remote_copy(ref, ref, insem.at[me], sem, device_id={"ctx": lax.rem(me + 1, n)}, device_id_type=MESH).wait_recv()

    def sent(sem):
        pltpu.make_async_remote_copy(kh, kh, sem, rdk, device_id={"ctx": lax.rem(me + 1, n)}, device_id_type=MESH).wait_send()

    pairs = [(kh, k, rk), (vh, v, rv), (qh, q, rq), (doh, do, rdo)]

    def part(which, dev, p):
        src, dst, _ = pairs[which]
        place = rows(me if p == 0 else 2 * n - 1 - me)
        own = pl.ds(p * half, half)
        return (src.at[dev, own], dst.at[place]) if which < 2 else (src.at[dev, :, own], dst.at[:, place])

    def give(which, dev, rel):
        for p in (0, 1):
            to(dev, *part(which, dev, p), insem, pairs[which][2].at[rel])

    other = me + 1 - 2 * lax.rem(me, 2)
    for which in range(4):
        for p in (0, 1):
            pltpu.make_async_copy(*part(which, me, p), pairs[which][2].at[0]).start()
        give(which, other, 0)
    for group, hops in (((0, 1), (1, 3, 2)), ((2, 3), (1, 3)), ((2, 3), (2,))):
        for which in group:
            for hop in hops:
                for core in (0, 1):
                    give(which, lax.rem(chip + hop, chips) * 2 + core, (chips - hop) % chips)

    def hand(ref, place, piece, sem):
        early = piece < n
        dev = jnp.where(early, piece, 2 * n - 1 - piece)
        own = pl.ds(pl.multiple_of(jnp.where(early, 0, half), half), half)
        src, dst = ref.at[rows(piece)], place.at[own]

        @pl.when(dev == me)
        def _():
            pltpu.make_async_copy(src, dst, sem).start()

        @pl.when(dev != me)
        def _():
            to(dev, src, dst, outsem, sem)

    def turn(src, dst, i, j):
        dst[:, at(j)] = src[at(i), :].T

    def phase(y, j, first, second, own, before, after):
        a, b = y, segs - 1 - y
        z = jnp.minimum(j, 0) * R
        diag = [(0, a, a), (1, b, b)]

        def full(t):
            if own:
                late = jnp.logical_or(t < 1, t > y)
                i = t - y - 1
                key = jnp.where(t < 1, a, jnp.where(late, jnp.where(i < a, i, i + 1), t - 1))
                return jnp.where(late, 1, 0), jnp.where(late, b, a), key
            early = t < y
            return jnp.where(early, 0, 1), jnp.where(early, a, b), jnp.where(early, t, t - y)

        def both(nxt, cur, z):
            carry = {}
            for r in range(nr):
                if nxt is not None:
                    first(*nxt, r, z)
                second(*cur, r, z, carry)

        for r in range(nr):
            first(True, diag[0], 0, r, z)
        order = [(True, d, h) for d in diag for h in range(heads)] + [(False, full(0), 0)]
        for cur, nxt in zip(order, order[1:]):
            both(nxt, cur, z)
        before()

        def loop(t, _):
            z = jnp.minimum(t, 0) * R
            now, later = full(t), full(t + 1)
            for h in range(heads):
                both((False, now, h + 1) if h + 1 < heads else (False, later, 0), (False, now, h), z)
            after(t)
            return 0

        lax.fori_loop(0, segs - 2, loop, 0)
        now = full(segs - 2)
        for h in range(heads):
            both((False, now, h + 1) if h + 1 < heads else None, (False, now, h), z)
        after(segs - 2)

    def span(z, c):
        return pl.ds(pl.multiple_of(z + c * R, R), R)

    def cols(sel, r):
        return pl.ds(pl.multiple_of(sel * seg + r * R, R), R)

    def fwd_a(diag, step, h, r, z):
        sel, qi, ki = step
        cs = slice(r * R, (r + 1) * R)
        m = None
        for c in range(r + 1 if diag else nr):
            x = dot(k[at(ki, c), :], qT[h, :, cols(sel, r)])
            if diag and c == r:
                x = jnp.where(triangle(True), x, NEG)
            sbs[h][span(z, c), cs] = x
            x = jnp.max(x, axis=0, keepdims=True)
            m = x if m is None else jnp.maximum(m, x)
        mbs[h][:, cs] = m

    def fwd_b(diag, step, h, r, z, carry):
        sel, qi, ki = step
        e = 2 * h + sel
        cs = slice(r * R, (r + 1) * R)
        m = mbs[h][:, cs] * c2
        if not diag:
            m = jnp.maximum(ms[e, :, cs], m)
        l = o = None
        for c in range(r + 1 if diag else nr):
            p = jnp.exp2(sbs[h][span(z, c), cs] * c2 - m)
            x, w = jnp.sum(p, axis=0, keepdims=True), dot(vT[:, at(ki, c)], p.astype(bf16))
            l, o = (x, w) if l is None else (l + x, o + w)
        if not diag:
            fade = jnp.exp2(ms[e, :, cs] - m)
            l = l + ls[e, :, cs] * fade
            o = o + acc[e, :, cs] * fade
        ms[e, :, cs] = m
        ls[e, :, cs] = l
        acc[e, :, cs] = o

    def bwd_a(diag, step, h, r, z):
        sel, qi, ki = step
        e = 2 * h + sel
        pb, db, tb = bufs[h]
        m = r + 1 if diag else nr
        w = m * R
        rs = slice(r * R, (r + 1) * R)
        s = dot(q[h, at(qi, r), :], kT[:, at(ki, 0, m)])
        dp = dot(do[h, at(qi, r), :], vT[:, at(ki, 0, m)])
        l = jnp.concatenate([lsc[e, rs, :]] * (w // 128), axis=1)
        d = jnp.concatenate([dsc[e, rs, :]] * (w // 128), axis=1)
        p = jnp.exp2(s * c2 - l)
        if diag:
            t = jnp.where(triangle(False), p[:, r * R:], 0.0)
            p = jnp.concatenate([p[:, :r * R], t], axis=1) if r else t
        ds = (p * (dp - d)).astype(bf16)
        pb[rs, :w] = p.astype(bf16)
        db[rs, :w] = ds
        tb[:w, rs] = ds.T

    def bwd_b(diag, step, h, r, z, carry):
        sel, qi, ki = step
        e = 2 * h + sel
        pb, db, tb = bufs[h]
        m = r + 1 if diag else nr
        w = m * R
        rs = slice(r * R, (r + 1) * R)
        ks = at(ki, 0, m)
        x = dot(doT[h, :, cols(sel, r)], pb[rs, :w])
        g = dot(qT[h, :, cols(sel, r)], db[rs, :w])
        u = dot(kT[:, ks], tb[:w, rs])
        if diag:
            acc[e, :, rs] = u
            dvT[:, ks] += x
            dkT[:, ks] += g
            return
        acc[e, :, rs] += u
        if r:
            x, g = carry["v"] + x, carry["k"] + g
        carry["v"], carry["k"] = x, g
        if r == nr - 1:
            dvT[:, ks] += x
            dkT[:, ks] += g

    def give_keys(i):
        k[at(i), :] = (dkT[:, at(i)] * scale).astype(bf16).T
        v[at(i), :] = dvT[:, at(i)].astype(bf16).T
        for p in (0, 1):
            hand(k, dko.at[me], 2 * i + p, rdk)
            hand(v, dvo.at[me], 2 * i + p, rdv)

    def give_queries(sel, i):
        for h in range(heads):
            q[h, at(i), :] = (acc[2 * h + sel] * scale).astype(bf16).T
        for h in range(heads):
            for p in (0, 1):
                hand(q.at[h], dqo.at[me, h], 2 * i + p, rdq)

    def set_of(j, _):
        rel = jnp.where(j == 2, 3, jnp.where(j == 3, 2, j))
        y = lax.rem(chip + rel, chips)
        a, b = y, segs - 1 - y
        last = j == chips - 1
        both = ((0, a), (1, b))

        def keys(r, ref, sem, out):
            arrived(ref.at[pl.ds(0, 2 * seg)], sem.at[r])
            x = lax.rem(chip + r, chips)
            for i in (x, segs - 1 - x):
                turn(ref, out, i, i)

        @pl.when(j == 0)
        def _():
            keys(0, k, rk, kT)
            keys(0, v, rv, vT)

        arrived(q.at[:, pl.ds(0, 2 * seg)], rq.at[rel])
        for h in range(heads):
            for sel, i in both:
                turn(q.at[h], qT.at[h], i, sel)

        def rest():
            @pl.when(j == 0)
            def _():
                for ref, sem, out in ((k, rk, kT), (v, rv, vT)):
                    def one(r, _):
                        keys(r, ref, sem, out)
                        return 0
                    lax.fori_loop(1, chips, one, 0)

        phase(y, j, fwd_a, fwd_b, True, rest, lambda t: None)
        for sel, i in both:
            for h in range(heads):
                e = 2 * h + sel
                l = ls[e]
                o = (acc[e] * (1.0 / l)).astype(bf16)
                oT[h, :, at(sel)] = o
                ob[h, at(i), :] = o.T
                lsc[e] = jnp.broadcast_to(ms[e] + jnp.log2(l), (128, seg)).T
        for sel, i in both:
            for h in range(heads):
                for p in (0, 1):
                    hand(ob.at[h], oo.at[me, h], 2 * i + p, ro)
        arrived(do.at[:, pl.ds(0, 2 * seg)], rdo.at[rel])
        for h in range(heads):
            for sel, i in both:
                g = do[h, at(i), :].T
                doT[h, :, at(sel)] = g
                d = jnp.sum(g.astype(f32) * oT[h, :, at(sel)].astype(f32), axis=0, keepdims=True)
                dsc[2 * h + sel] = jnp.broadcast_to(d, (128, seg)).T

        def ready():
            @pl.when(last)
            def _():
                def one(i, _):
                    give_keys(i)
                    return 0
                lax.fori_loop(b, segs, one, 0)

        def done(t):
            @pl.when(jnp.logical_and(last, t >= y))
            def _():
                give_keys(t - y)

            @pl.when(t == y)
            def _():
                give_queries(0, a)

        phase(y, j, bwd_a, bwd_b, False, ready, done)
        give_queries(1, b)
        return 0

    dkT[...] = jnp.zeros_like(dkT)
    dvT[...] = jnp.zeros_like(dvT)
    lax.fori_loop(0, chips, set_of, 0)
    for off in range(1, n):
        sent(insem.at[lax.rem(me + off, n)])
        sent(outsem.at[lax.rem(me + off, n)])
    arrived(oo, ro)
    arrived(dqo, rdq)
    arrived(dko, rdk)
    arrived(dvo, rdv)


def solution(mesh):
    n = mesh.shape["ctx"]
    spec = P("data", "ctx", None, None)

    def local(queries, keys_in, values_in, grad_out):
        batch, shard, heads, dim = queries.shape
        assert batch == n and keys_in.shape[2] == 1
        seq = n * shard
        q, g = (t.transpose(0, 2, 1, 3) for t in (queries, grad_out))
        k, v = (t.reshape(batch, shard, dim) for t in (keys_in, values_in))
        hbm = pl.BlockSpec(memory_space=pl.ANY)
        vm, dma = pltpu.VMEM, pltpu.SemaphoreType.DMA
        wide = jax.ShapeDtypeStruct(q.shape, bf16)
        thin = jax.ShapeDtypeStruct(k.shape, bf16)
        o, dq, dk, dv = pl.pallas_call(
            functools.partial(kernel, n),
            out_shape=[wide, wide, thin, thin],
            in_specs=[hbm] * 4,
            out_specs=[hbm] * 4,
            scratch_shapes=[vm((heads, seq, dim), bf16)] * 3 + [vm((seq, dim), bf16)] * 2 + [vm((dim, seq), bf16)] * 2
            + [vm((heads, dim, 2 * shard), bf16)] * 3
            + [vm((2 * heads, dim, shard), f32), vm((2 * heads, 1, shard), f32), vm((2 * heads, 1, shard), f32)]
            + [vm((2 * heads, shard, 128), f32)] * 2 + [vm((dim, seq), f32)] * 2
            + [vm((shard, shard), f32)] * 3 + [vm((1, shard), f32)] * 3 + [vm((shard, shard), bf16)] * 9
            + [dma((n,)), dma((n,))] + [dma((n // 2,))] * 4 + [dma] * 4,
            compiler_params=pltpu.CompilerParams(collective_id=0, has_side_effects=True, vmem_limit_bytes=67043328),
            name="attention",
        )(q, g, k, v)
        o, dq = (t.transpose(0, 2, 1, 3) for t in (o, dq))
        dk, dv = (t.reshape(keys_in.shape) for t in (dk, dv))
        return o, dq, dk, dv

    return jax.shard_map(local, mesh=mesh, in_specs=(spec,) * 4, out_specs=(spec,) * 4, check_vma=False)
```

time: 2230 us -> 312 us (0.14); the launches traced: 2190 us -> 312 us
  waiting for transfers between devices: 969 us -> 0 us
  matrix products: 829 us -> 0 us
  Pallas kernels: 0 us -> 301 us
  other arithmetic: 230 us -> 0 us
  local copies, waits for them, and re-layouts: 124 us -> 10.1 us
  starting transfers between devices: 34.7 us -> 0 us
    ppermute x44 -> x0, waiting for transfers between devices: 969 us -> none  [the longest x7 592 us: bwd_step(): k_cur = lax.ppermute(k_cur, 'ctx', perm_next)]
    dot_general x55 -> x0, matrix products: 829 us -> none  [the longest x15 224 us: scores_of(): jnp.einsum('bqhgd,bkhd->bhgqk', q_blk, k_blk, preferred_element_type=jnp....]
    pallas_call x0 -> x1, Pallas kernels: none -> 301 us  [local(): pl.pallas_call(functools.partial(kernel, n), out_shape=[wide, wide, thin,...]
    reduce_sum x8 -> x0, other arithmetic: 105 us -> none  [fwd_update(): new_sum = run_sum * decay_factor + jnp.sum(prob_tile, axis=-1)]
    concatenate x19 -> x0, other arithmetic: 99 us -> none  [the longest x12 54.2 us: fwd_future(): jnp.concatenate([low_part, high_part], axis=3)]
    while x35 -> x0, local copies, waits for them, and re-layouts: 70.5 us -> none
    slice x14 -> x0, local copies, waits for them, and re-layouts: 36.5 us -> none  [the longest x6 17.6 us: bwd_future(): dq_acc[:, :half_len]]
    ppermute x44 -> x0, starting transfers between devices: 34.7 us -> none  [the longest x7 15.2 us: fwd_step(): k_cur = lax.ppermute(k_cur, 'ctx', perm_next)]
  transfers between devices with their start and end apart: 44 -> 0, of which waited for: 30 -> 0; matrix products, arithmetic and copies ran while one was open for 2% -> 0% of each run, Pallas kernels for 0% -> 0%
where the time goes in v2:
time: 312 us
  Pallas kernels  301 us (96%)
  local copies, waits for them, and re-layouts  10.1 us (3%)
    pallas_call x1, Pallas kernels, local(): pl.pallas_call(functools.partial(kernel, n), out_shape=[wide, wide, thin,...  301 us
    unnamed x10, local copies, waits for them, and re-layouts  10.1 us

profile of v2, /device:TPU:81, one launch (start us, length us, event | category | flops | bytes accessed | tf_op | source)
XLA Modules:
  0.0 312.0 jit_solution(10520921209087702369)
XLA Ops:
  0.6 301.3 %attention.1 = (bf16[8,3,768,128]{3,2,1,0:T(8,128)(2,1)}, bf16[8,3,768,128]{3,2,1,0:T(8,128)(2,1)}, bf16[8,768,128]{2,1,0:T(8,128)(2,1)}, bf16[8,768,128]{2,1,0:T(8,128)(2,1)}) custom-call(bf16[8,3,768,128]{3,2,1,0:T(8,128)(2,1)} %bitcast.12, bf16[8,3,768,128]{3,2,1,0:T(8,128)(2,1)} %bitcast.13, bf16[8,768,128]{2,1,0:T(8,128)(2,1)} %bitcast.16, ...), custom_call_target="tpu_custom_call" | custom-call | tf_op jit(solution)/shard_map/attention/pallas_call | solution.py:338
  301.9 0.0 copy-start
  301.9 5.1 %copy.14 = bf16[8,768,3,128]{3,1,2,0:T(8,128)(2,1)} copy(bf16[8,768,3,128]{3,1,2,0:T(8,128)(2,1)} %bitcast.15) | data formatting | bytes 9437184
  307.1 0.0 copy-done
  307.1 0.0 copy-start.2
  307.1 0.0 copy-start.1
  307.1 2.4 copy.15
  309.5 0.1 copy-done.2
  309.6 1.1 copy.16
  310.7 0.1 copy-done.1
  310.9 1.1 copy.17
Async XLA Ops:
  301.9 5.1 %copy-start = (bf16[8,3,768,128]{3,2,1,0:T(8,128)(2,1)S(1)}, bf16[8,3,768,128]{3,2,1,0:T(8,128)(2,1)}, u32[]{:S(2)}) copy-start(bf16[8,3,768,128]{3,2,1,0:T(8,128)(2,1)} %get-tuple-element.9) | copy-start | bytes 14155780
  307.1 2.5 copy-start.2
  307.1 3.8 %copy-start.1 = (bf16[8,768,128]{2,1,0:T(8,128)(2,1)S(1)}, bf16[8,768,128]{2,1,0:T(8,128)(2,1)}, u32[]{:S(2)}) copy-start(bf16[8,768,128]{2,1,0:T(8,128)(2,1)} %get-tuple-element.11) | copy-start | bytes 4718596

commit v3 on v2

--- a/solution.py
+++ b/solution.py
@@ -23,7 +23,7 @@
     return i <= j if flip else i >= j
 
 
-def kernel(n, qh, doh, kh, vh, oo, dqo, dko, dvo, q, do, ob, k, v, kT, vT, qT, doT, oT, acc, ms, ls, lsc, dsc, dkT, dvT,
+def kernel(n, qh, doh, kh, vh, oo, dqo, dko, dvo, q, do, ob, k, v, kT, vT, qT, doT, acc, ms, ls, lse, lsc, dsc, dkT, dvT,
            sb0, sb1, sb2, mb0, mb1, mb2, pb0, pb1, pb2, db0, db1, db2, tb0, tb1, tb2, insem, outsem, rk, rv, rq, rdo, ro, rdq, rdk, rdv):
     heads, shard, dim = qh.shape[1:]
     half, seg, segs, chips = shard // 2, shard, n, n // 2
@@ -64,20 +64,23 @@
         own = pl.ds(p * half, half)
         return (src.at[dev, own], dst.at[place]) if which < 2 else (src.at[dev, :, own], dst.at[:, place])
 
-    def give(which, dev, rel):
-        for p in (0, 1):
-            to(dev, *part(which, dev, p), insem, pairs[which][2].at[rel])
+    def landing(which, rel, p):
+        return pairs[which][2].at[p * chips + rel] if which < 2 else pairs[which][2].at[rel]
+
+    def give(which, dev, rel, halves=(0, 1)):
+        for p in halves:
+            to(dev, *part(which, dev, p), insem, landing(which, rel, p))
 
     other = me + 1 - 2 * lax.rem(me, 2)
     for which in range(4):
         for p in (0, 1):
-            pltpu.make_async_copy(*part(which, me, p), pairs[which][2].at[0]).start()
+            pltpu.make_async_copy(*part(which, me, p), landing(which, 0, p)).start()
         give(which, other, 0)
-    for group, hops in (((0, 1), (1, 3, 2)), ((2, 3), (1, 3)), ((2, 3), (2,))):
+    for group, hops, halves in (((0, 1), (1, 3, 2), (0,)), ((0, 1), (1, 3, 2), (1,)), ((2, 3), (1, 3), (0, 1)), ((2, 3), (2,), (0, 1))):
         for which in group:
             for hop in hops:
                 for core in (0, 1):
-                    give(which, lax.rem(chip + hop, chips) * 2 + core, (chips - hop) % chips)
+                    give(which, lax.rem(chip + hop, chips) * 2 + core, (chips - hop) % chips, halves)
 
     def hand(ref, place, piece, sem):
         early = piece < n
@@ -129,10 +132,14 @@
             now, later = full(t), full(t + 1)
             for h in range(heads):
                 both((False, now, h + 1) if h + 1 < heads else (False, later, 0), (False, now, h), z)
-            after(t)
+
+        def two(i, _):
+            loop(2 * i, 0)
+            loop(2 * i + 1, 0)
+            after(2 * i)
             return 0
 
-        lax.fori_loop(0, segs - 2, loop, 0)
+        lax.fori_loop(0, (segs - 2) // 2, two, 0)
         now = full(segs - 2)
         for h in range(heads):
             both((False, now, h + 1) if h + 1 < heads else None, (False, now, h), z)
@@ -235,58 +242,70 @@
             for p in (0, 1):
                 hand(q.at[h], dqo.at[me, h], 2 * i + p, rdq)
 
-    def set_of(j, _):
+    def keys(rel, p):
+        x = lax.rem(chip + rel, chips)
+        i = x if p == 0 else segs - 1 - x
+        for ref, sem, out in ((k, rk, kT), (v, rv, vT)):
+            arrived(ref.at[pl.ds(0, seg)], sem.at[p * chips + rel])
+            turn(ref, out, i, i)
+
+    def others(p):
+        def one(rel, _):
+            keys(rel, p)
+            return 0
+
+        lax.fori_loop(1, chips, one, 0)
+
+    def place(j):
         rel = jnp.where(j == 2, 3, jnp.where(j == 3, 2, j))
         y = lax.rem(chip + rel, chips)
         a, b = y, segs - 1 - y
-        last = j == chips - 1
-        both = ((0, a), (1, b))
-
-        def keys(r, ref, sem, out):
-            arrived(ref.at[pl.ds(0, 2 * seg)], sem.at[r])
-            x = lax.rem(chip + r, chips)
-            for i in (x, segs - 1 - x):
-                turn(ref, out, i, i)
-
-        @pl.when(j == 0)
-        def _():
-            keys(0, k, rk, kT)
-            keys(0, v, rv, vT)
-
-        arrived(q.at[:, pl.ds(0, 2 * seg)], rq.at[rel])
+        return rel, y, a, b, ((0, a), (1, b))
+
+    def turn_queries(both):
         for h in range(heads):
             for sel, i in both:
                 turn(q.at[h], qT.at[h], i, sel)
 
-        def rest():
+    def forward(j):
+        rel, y, a, b, both = place(j)
+        arrived(q.at[:, pl.ds(0, 2 * seg)], rq.at[rel])
+        turn_queries(both)
+
+        def low():
             @pl.when(j == 0)
             def _():
-                for ref, sem, out in ((k, rk, kT), (v, rv, vT)):
-                    def one(r, _):
-                        keys(r, ref, sem, out)
-                        return 0
-                    lax.fori_loop(1, chips, one, 0)
-
-        phase(y, j, fwd_a, fwd_b, True, rest, lambda t: None)
+                others(0)
+
+        def high(t):
+            @pl.when(jnp.logical_and(j == 0, t == (y + 1) // 2 * 2))
+            def _():
+                others(1)
+
+        phase(y, j, fwd_a, fwd_b, True, low, high)
         for sel, i in both:
             for h in range(heads):
                 e = 2 * h + sel
                 l = ls[e]
-                o = (acc[e] * (1.0 / l)).astype(bf16)
-                oT[h, :, at(sel)] = o
-                ob[h, at(i), :] = o.T
-                lsc[e] = jnp.broadcast_to(ms[e] + jnp.log2(l), (128, seg)).T
+                ob[h, at(i), :] = (acc[e] * (1.0 / l)).astype(bf16).T
+                lse[j, e] = ms[e] + jnp.log2(l)
         for sel, i in both:
             for h in range(heads):
                 for p in (0, 1):
                     hand(ob.at[h], oo.at[me, h], 2 * i + p, ro)
+
+    def backward(j, last):
+        rel, y, a, b, both = place(j)
         arrived(do.at[:, pl.ds(0, 2 * seg)], rdo.at[rel])
+        turn_queries(both)
         for h in range(heads):
             for sel, i in both:
-                g = do[h, at(i), :].T
-                doT[h, :, at(sel)] = g
-                d = jnp.sum(g.astype(f32) * oT[h, :, at(sel)].astype(f32), axis=0, keepdims=True)
-                dsc[2 * h + sel] = jnp.broadcast_to(d, (128, seg)).T
+                e = 2 * h + sel
+                turn(do.at[h], doT.at[h], i, sel)
+                lsc[e] = jnp.broadcast_to(lse[j, e], (128, seg)).T
+                for r in range(nr):
+                    d = jnp.sum(do[h, at(i, r), :].astype(f32) * ob[h, at(i, r), :].astype(f32), axis=1, keepdims=True)
+                    dsc[e, r * R:(r + 1) * R, :] = jnp.broadcast_to(d, (R, 128))
 
         def ready():
             @pl.when(last)
@@ -294,24 +313,41 @@
                 def one(i, _):
                     give_keys(i)
                     return 0
+
                 lax.fori_loop(b, segs, one, 0)
 
         def done(t):
-            @pl.when(jnp.logical_and(last, t >= y))
-            def _():
-                give_keys(t - y)
-
-            @pl.when(t == y)
-            def _():
-                give_queries(0, a)
+            for i in (t, t + 1) if t is not segs - 2 else (t,):
+                @pl.when(jnp.logical_and(last, i >= y))
+                def _():
+                    give_keys(i - y)
+
+                @pl.when(i == y)
+                def _():
+                    give_queries(0, a)
 
         phase(y, j, bwd_a, bwd_b, False, ready, done)
         give_queries(1, b)
+
+    def turns(s, _):
+        is_f = jnp.logical_or(s < 3, s == 4)
+        j = jnp.where(s < 3, s, jnp.where(s == 3, 1, jnp.where(s < 6, 3, jnp.where(s == 6, 2, 0))))
+
+        @pl.when(is_f)
+        def _():
+            forward(j)
+
+        @pl.when(jnp.logical_not(is_f))
+        def _():
+            backward(j, s == 7)
+
         return 0
 
     dkT[...] = jnp.zeros_like(dkT)
     dvT[...] = jnp.zeros_like(dvT)
-    lax.fori_loop(0, chips, set_of, 0)
+    keys(0, 0)
+    keys(0, 1)
+    lax.fori_loop(0, 2 * chips, turns, 0)
     for off in range(1, n):
         sent(insem.at[lax.rem(me + off, n)])
         sent(outsem.at[lax.rem(me + off, n)])
@@ -341,11 +377,11 @@
             in_specs=[hbm] * 4,
             out_specs=[hbm] * 4,
             scratch_shapes=[vm((heads, seq, dim), bf16)] * 3 + [vm((seq, dim), bf16)] * 2 + [vm((dim, seq), bf16)] * 2
-            + [vm((heads, dim, 2 * shard), bf16)] * 3
-            + [vm((2 * heads, dim, shard), f32), vm((2 * heads, 1, shard), f32), vm((2 * heads, 1, shard), f32)]
+            + [vm((heads, dim, 2 * shard), bf16)] * 2
+            + [vm((2 * heads, dim, shard), f32), vm((2 * heads, 1, shard), f32), vm((2 * heads, 1, shard), f32), vm((n // 2, 2 * heads, 1, shard), f32)]
             + [vm((2 * heads, shard, 128), f32)] * 2 + [vm((dim, seq), f32)] * 2
             + [vm((shard, shard), f32)] * 3 + [vm((1, shard), f32)] * 3 + [vm((shard, shard), bf16)] * 9
-            + [dma((n,)), dma((n,))] + [dma((n // 2,))] * 4 + [dma] * 4,
+            + [dma((n,)), dma((n,)), dma((n,)), dma((n,)), dma((n // 2,)), dma((n // 2,))] + [dma] * 4,
             compiler_params=pltpu.CompilerParams(collective_id=0, has_side_effects=True, vmem_limit_bytes=67043328),
             name="attention",
         )(q, g, k, v)

time: 312 us -> 289 us (0.926)
  Pallas kernels: 301 us -> 278 us
    pallas_call x1, Pallas kernels: 301 us -> 278 us  [local(): pl.pallas_call(functools.partial(kernel, n), out_shape=[wide, wide, thin,...]
where the time goes in v3:
time: 289 us
  Pallas kernels  278 us (96%)
  local copies, waits for them, and re-layouts  10.1 us (3%)
    pallas_call x1, Pallas kernels, local(): pl.pallas_call(functools.partial(kernel, n), out_shape=[wide, wide, thin,...  278 us
    unnamed x10, local copies, waits for them, and re-layouts  10.1 us

profile of v3, /device:TPU:81, one launch (start us, length us, event | category | flops | bytes accessed | tf_op | source)
XLA Modules:
  0.0 288.6 jit_solution(5031867694647120755)
XLA Ops:
  0.6 277.9 %attention.1 = (bf16[8,3,768,128]{3,2,1,0:T(8,128)(2,1)}, bf16[8,3,768,128]{3,2,1,0:T(8,128)(2,1)}, bf16[8,768,128]{2,1,0:T(8,128)(2,1)}, bf16[8,768,128]{2,1,0:T(8,128)(2,1)}) custom-call(bf16[8,3,768,128]{3,2,1,0:T(8,128)(2,1)} %bitcast.12, bf16[8,3,768,128]{3,2,1,0:T(8,128)(2,1)} %bitcast.13, bf16[8,768,128]{2,1,0:T(8,128)(2,1)} %bitcast.16, ...), custom_call_target="tpu_custom_call" | custom-call | tf_op jit(solution)/shard_map/attention/pallas_call | solution.py:374
  278.5 0.0 copy-start
  278.5 5.1 %copy.14 = bf16[8,768,3,128]{3,1,2,0:T(8,128)(2,1)} copy(bf16[8,768,3,128]{3,1,2,0:T(8,128)(2,1)} %bitcast.15) | data formatting | bytes 9437184
  283.6 0.0 copy-done
  283.7 0.0 copy-start.2
  283.7 0.0 copy-start.1
  283.7 2.4 copy.15
  286.1 0.1 copy-done.2
  286.2 1.1 copy.16
  287.3 0.1 copy-done.1
  287.4 1.1 copy.17
Async XLA Ops:
  278.5 5.1 %copy-start = (bf16[8,3,768,128]{3,2,1,0:T(8,128)(2,1)S(1)}, bf16[8,3,768,128]{3,2,1,0:T(8,128)(2,1)}, u32[]{:S(2)}) copy-start(bf16[8,3,768,128]{3,2,1,0:T(8,128)(2,1)} %get-tuple-element.9) | copy-start | bytes 14155780
  283.7 2.5 copy-start.2
  283.7 3.8 %copy-start.1 = (bf16[8,768,128]{2,1,0:T(8,128)(2,1)S(1)}, bf16[8,768,128]{2,1,0:T(8,128)(2,1)}, u32[]{:S(2)}) copy-start(bf16[8,768,128]{2,1,0:T(8,128)(2,1)} %get-tuple-element.11) | copy-start | bytes 4718596

commit v4 on v3

--- a/solution.py
+++ b/solution.py
@@ -24,11 +24,11 @@
 
 
 def kernel(n, qh, doh, kh, vh, oo, dqo, dko, dvo, q, do, ob, k, v, kT, vT, qT, doT, acc, ms, ls, lse, lsc, dsc, dkT, dvT,
-           sb0, sb1, sb2, mb0, mb1, mb2, pb0, pb1, pb2, db0, db1, db2, tb0, tb1, tb2, insem, outsem, rk, rv, rq, rdo, ro, rdq, rdk, rdv):
+           sb0, sb1, mb0, mb1, pb0, pb1, db0, db1, tb0, tb1, insem, outsem, rk, rv, rq, rdo, ro, rdq, rdk, rdv):
     heads, shard, dim = qh.shape[1:]
     half, seg, segs, chips = shard // 2, shard, n, n // 2
     nr = seg // R
-    sbs, mbs, bufs = (sb0, sb1, sb2), (mb0, mb1, mb2), ((pb0, db0, tb0), (pb1, db1, tb1), (pb2, db2, tb2))
+    sbs, mbs, bufs = (sb0, sb1), (mb0, mb1), ((pb0, db0, tb0), (pb1, db1, tb1))
     me = lax.axis_index("ctx")
     chip = me // 2
     scale = dim ** -0.5
@@ -113,36 +113,36 @@
             early = t < y
             return jnp.where(early, 0, 1), jnp.where(early, a, b), jnp.where(early, t, t - y)
 
-        def both(nxt, cur, z):
+        def both(nxt, cur, slot, z):
             carry = {}
             for r in range(nr):
                 if nxt is not None:
-                    first(*nxt, r, z)
-                second(*cur, r, z, carry)
+                    first(*nxt, 1 - slot, r, z)
+                second(*cur, slot, r, z, carry)
 
         for r in range(nr):
-            first(True, diag[0], 0, r, z)
+            first(True, diag[0], 0, 0, r, z)
         order = [(True, d, h) for d in diag for h in range(heads)] + [(False, full(0), 0)]
-        for cur, nxt in zip(order, order[1:]):
-            both(nxt, cur, z)
+        for i, (cur, nxt) in enumerate(zip(order, order[1:])):
+            both(nxt, cur, i % 2, z)
         before()
 
-        def loop(t, _):
+        def loop(t, odd):
             z = jnp.minimum(t, 0) * R
             now, later = full(t), full(t + 1)
             for h in range(heads):
-                both((False, now, h + 1) if h + 1 < heads else (False, later, 0), (False, now, h), z)
+                both((False, now, h + 1) if h + 1 < heads else (False, later, 0), (False, now, h), (2 * heads + heads * odd + h) % 2, z)
 
         def two(i, _):
             loop(2 * i, 0)
-            loop(2 * i + 1, 0)
+            loop(2 * i + 1, 1)
             after(2 * i)
             return 0
 
         lax.fori_loop(0, (segs - 2) // 2, two, 0)
         now = full(segs - 2)
         for h in range(heads):
-            both((False, now, h + 1) if h + 1 < heads else None, (False, now, h), z)
+            both((False, now, h + 1) if h + 1 < heads else None, (False, now, h), (2 * heads + heads * (segs - 2) + h) % 2, z)
         after(segs - 2)
 
     def span(z, c):
@@ -151,7 +151,7 @@
     def cols(sel, r):
         return pl.ds(pl.multiple_of(sel * seg + r * R, R), R)
 
-    def fwd_a(diag, step, h, r, z):
+    def fwd_a(diag, step, h, slot, r, z):
         sel, qi, ki = step
         cs = slice(r * R, (r + 1) * R)
         m = None
@@ -159,21 +159,21 @@
             x = dot(k[at(ki, c), :], qT[h, :, cols(sel, r)])
             if diag and c == r:
                 x = jnp.where(triangle(True), x, NEG)
-            sbs[h][span(z, c), cs] = x
+            sbs[slot][span(z, c), cs] = x
             x = jnp.max(x, axis=0, keepdims=True)
             m = x if m is None else jnp.maximum(m, x)
-        mbs[h][:, cs] = m
-
-    def fwd_b(diag, step, h, r, z, carry):
+        mbs[slot][:, cs] = m
+
+    def fwd_b(diag, step, h, slot, r, z, carry):
         sel, qi, ki = step
         e = 2 * h + sel
         cs = slice(r * R, (r + 1) * R)
-        m = mbs[h][:, cs] * c2
+        m = mbs[slot][:, cs] * c2
         if not diag:
             m = jnp.maximum(ms[e, :, cs], m)
         l = o = None
         for c in range(r + 1 if diag else nr):
-            p = jnp.exp2(sbs[h][span(z, c), cs] * c2 - m)
+            p = jnp.exp2(sbs[slot][span(z, c), cs] * c2 - m)
             x, w = jnp.sum(p, axis=0, keepdims=True), dot(vT[:, at(ki, c)], p.astype(bf16))
             l, o = (x, w) if l is None else (l + x, o + w)
         if not diag:
@@ -184,10 +184,10 @@
         ls[e, :, cs] = l
         acc[e, :, cs] = o
 
-    def bwd_a(diag, step, h, r, z):
+    def bwd_a(diag, step, h, slot, r, z):
         sel, qi, ki = step
         e = 2 * h + sel
-        pb, db, tb = bufs[h]
+        pb, db, tb = bufs[slot]
         m = r + 1 if diag else nr
         w = m * R
         rs = slice(r * R, (r + 1) * R)
@@ -204,10 +204,10 @@
         db[rs, :w] = ds
         tb[:w, rs] = ds.T
 
-    def bwd_b(diag, step, h, r, z, carry):
+    def bwd_b(diag, step, h, slot, r, z, carry):
         sel, qi, ki = step
         e = 2 * h + sel
-        pb, db, tb = bufs[h]
+        pb, db, tb = bufs[slot]
         m = r + 1 if diag else nr
         w = m * R
         rs = slice(r * R, (r + 1) * R)
@@ -357,6 +357,18 @@
     arrived(dvo, rdv)
 
 
+def store(*refs):
+    sem = refs[-1]
+    copies = []
+    for i in range(4):
+        for b in range(refs[i].shape[0]):
+            copies.append(pltpu.make_async_copy(refs[i].at[b], refs[4 + i].at[b], sem.at[i, b]))
+    for copy in copies:
+        copy.start()
+    for copy in copies:
+        copy.wait()
+
+
 def solution(mesh):
     n = mesh.shape["ctx"]
     spec = P("data", "ctx", None, None)
@@ -369,22 +381,30 @@
         k, v = (t.reshape(batch, shard, dim) for t in (keys_in, values_in))
         hbm = pl.BlockSpec(memory_space=pl.ANY)
         vm, dma = pltpu.VMEM, pltpu.SemaphoreType.DMA
-        wide = jax.ShapeDtypeStruct(q.shape, bf16)
-        thin = jax.ShapeDtypeStruct(k.shape, bf16)
-        o, dq, dk, dv = pl.pallas_call(
+        wide, thin = vm(q.shape, bf16), vm(k.shape, bf16)
+        results = pl.pallas_call(
             functools.partial(kernel, n),
             out_shape=[wide, wide, thin, thin],
             in_specs=[hbm] * 4,
-            out_specs=[hbm] * 4,
+            out_specs=[pl.BlockSpec(memory_space=pltpu.VMEM)] * 4,
             scratch_shapes=[vm((heads, seq, dim), bf16)] * 3 + [vm((seq, dim), bf16)] * 2 + [vm((dim, seq), bf16)] * 2
             + [vm((heads, dim, 2 * shard), bf16)] * 2
             + [vm((2 * heads, dim, shard), f32), vm((2 * heads, 1, shard), f32), vm((2 * heads, 1, shard), f32), vm((n // 2, 2 * heads, 1, shard), f32)]
             + [vm((2 * heads, shard, 128), f32)] * 2 + [vm((dim, seq), f32)] * 2
-            + [vm((shard, shard), f32)] * 3 + [vm((1, shard), f32)] * 3 + [vm((shard, shard), bf16)] * 9
+            + [vm((shard, shard), f32)] * 2 + [vm((1, shard), f32)] * 2 + [vm((shard, shard), bf16)] * 6
             + [dma((n,)), dma((n,)), dma((n,)), dma((n,)), dma((n // 2,)), dma((n // 2,))] + [dma] * 4,
-            compiler_params=pltpu.CompilerParams(collective_id=0, has_side_effects=True, vmem_limit_bytes=67043328),
+            compiler_params=pltpu.CompilerParams(collective_id=0, has_side_effects=True, vmem_limit_bytes=54400000),
             name="attention",
         )(q, g, k, v)
+        o, dq, dk, dv = pl.pallas_call(
+            store,
+            out_shape=[jax.ShapeDtypeStruct(t.shape, bf16) for t in results],
+            in_specs=[hbm] * 4,
+            out_specs=[pl.BlockSpec(memory_space=pltpu.HBM)] * 4,
+            scratch_shapes=[dma((4, batch))],
+            compiler_params=pltpu.CompilerParams(vmem_limit_bytes=1 << 20),
+            name="store",
+        )(*results)
         o, dq = (t.transpose(0, 2, 1, 3) for t in (o, dq))
         dk, dv = (t.reshape(keys_in.shape) for t in (dk, dv))
         return o, dq, dk, dv

time: 289 us -> 285 us (0.986)
  local copies, waits for them, and re-layouts: 10.1 us -> 0 us
  Pallas kernels: 278 us -> 284 us
    unnamed x10 -> x0, local copies, waits for them, and re-layouts: 10.1 us -> none
    pallas_call x0 -> x1, Pallas kernels: none -> 4.82 us  [local(): pl.pallas_call(store, out_shape=[jax.ShapeDtypeStruct(t.shape, bf16) for...]
where the time goes in v4:
time: 285 us
  Pallas kernels  284 us (100%)
    pallas_call x1, Pallas kernels, local(): pl.pallas_call(functools.partial(kernel, n), out_shape=[wide, wide, thin,...  279 us

profile of v4, /device:TPU:81, one launch (start us, length us, event | category | flops | bytes accessed | tf_op | source)
XLA Modules:
  0.0 284.6 jit_solution(1839088692557098593)
XLA Ops:
  0.6 279.1 %attention.1 = (bf16[8,3,768,128]{3,2,1,0:T(8,128)(2,1)S(1)}, bf16[8,3,768,128]{3,2,1,0:T(8,128)(2,1)S(1)}, bf16[8,768,128]{2,1,0:T(8,128)(2,1)S(1)}, bf16[8,768,128]{2,1,0:T(8,128)(2,1)S(1)}) custom-call(bf16[8,3,768,128]{3,2,1,0:T(8,128)(2,1)} %bitcast.12, bf16[8,3,768,128]{3,2,1,0:T(8,128)(2,1)} %bitcast.13, bf16[8,768,128]{2,1,0:T(8,128)(2,1)} %bitcast.14, ...), custom_call_target="tpu_custom_call" | custom-call | tf_op jit(solution)/shard_map/attention/pallas_call | solution.py:385
  279.8 4.8 %store.1 = (bf16[8,3,768,128]{3,2,1,0:T(8,128)(2,1)}, bf16[8,3,768,128]{3,2,1,0:T(8,128)(2,1)}, bf16[8,768,128]{2,1,0:T(8,128)(2,1)}, bf16[8,768,128]{2,1,0:T(8,128)(2,1)}) custom-call(bf16[8,3,768,128]{3,2,1,0:T(8,128)(2,1)S(1)} %get-tuple-element.12.refs_0_, bf16[8,3,768,128]{3,2,1,0:T(8,128)(2,1)S(1)} %get-tuple-element.13.refs_1_, ...), custom_call_target="tpu_custom_call" | custom-call | tf_op jit(solution)/shard_map/store/pallas_call | solution.py:399
